TPU v7x, 32 devices: a 4x4x1 block of a 4x4x8 slice. The times are simulated.
32 devices in a mesh: rep: 1 (over z), dp: 4 (over y), sp: 8 (over x, core).
Axes of the slice: x: 4, y: 4, z: 1, core: 2. Of those that a mesh axis runs over, the one named last changes fastest.
The devices are a block of a 4x4x8 slice.
Arguments:
- hidden: bfloat16 [32, 3584], P(('rep', 'dp'))
- w_query: bfloat16 [3584, 4096], replicated
- w_key: bfloat16 [3584, 2048], replicated
- w_value: bfloat16 [3584, 2048], replicated
- w_out: bfloat16 [4096, 3584], P('sp')
- k_cache: bfloat16 [32, 2048, 8, 256], P(('rep', 'dp'), 'sp')
- v_cache: bfloat16 [32, 2048, 8, 256], P(('rep', 'dp'), 'sp')
- write_pos: int32 [32], P(('rep', 'dp'))
- valid_len: int32 [32], P(('rep', 'dp'))
Outputs:
- output 1: bfloat16 [32, 3584], P(('rep', 'dp'))
- output 2: bfloat16 [32, 2048, 8, 256], P(('rep', 'dp'), 'sp')
- output 3: bfloat16 [32, 2048, 8, 256], P(('rep', 'dp'), 'sp')
All inputs are finite; a program needn't handle non-finite values.
Results may differ from a plain program's by a relative error of at most 0.00646443.
Values are sent between devices in bfloat16 or wider.
A program may use at most 768 MiB of HBM per device.

v0:
```python
import jax
import jax.numpy as jnp
from jax import lax
from jax.sharding import PartitionSpec as P

NEG_FLOOR = -1e30


def solution(mesh):
    row_spec = P(('rep', 'dp'), None)
    cache_spec = P(('rep', 'dp'), 'sp', None, None)
    len_spec = P(('rep', 'dp'))

    def local_step(hidden, w_query, w_key, w_value, w_out, k_cache, v_cache, write_pos, valid_len):
        num_rows, seq_local, kv_heads, head_dim = k_cache.shape
        num_heads = w_query.shape[1] // head_dim
        group_size = num_heads // kv_heads
        shard_idx = lax.axis_index('sp')
        query = jnp.dot(hidden, w_query, preferred_element_type=jnp.float32).astype(jnp.bfloat16)
        query = query.reshape(num_rows, kv_heads, group_size, head_dim)
        key_new = jnp.dot(hidden, w_key, preferred_element_type=jnp.float32).astype(jnp.bfloat16)
        value_new = jnp.dot(hidden, w_value, preferred_element_type=jnp.float32).astype(jnp.bfloat16)
        positions = shard_idx * seq_local + jnp.arange(seq_local, dtype=jnp.int32)
        at_pos = (positions[None, :] == write_pos[:, None])[:, :, None, None]
        k_next = jnp.where(at_pos, key_new.reshape(num_rows, 1, kv_heads, head_dim), k_cache)
        v_next = jnp.where(at_pos, value_new.reshape(num_rows, 1, kv_heads, head_dim), v_cache)
        scores = jnp.einsum('bkgd,bskd->bkgs', query, k_next, preferred_element_type=jnp.float32) * head_dim ** -0.5
        valid_mask = (positions[None, :] < valid_len[:, None])[:, None, None, :]
        scores = jnp.where(valid_mask, scores, -jnp.inf)
        local_max = jnp.maximum(jnp.max(scores, axis=-1), NEG_FLOOR)
        weights = jnp.exp(scores - local_max[..., None])
        local_sum = jnp.sum(weights, axis=-1)
        local_acc = jnp.einsum('bkgs,bskd->bkgd', weights.astype(jnp.bfloat16), v_next, preferred_element_type=jnp.float32)
        global_max = lax.pmax(local_max, 'sp')
        rescale = jnp.exp(local_max - global_max)
        packed = jnp.concatenate([local_acc * rescale[..., None], (local_sum * rescale)[..., None]], axis=-1)
        packed = lax.psum(packed, 'sp')
        attention = (packed[..., :head_dim] / packed[..., head_dim:]).astype(jnp.bfloat16)
        attention = attention.reshape(num_rows, num_heads * head_dim)
        out_rows = w_out.shape[0]
        attn_mine = lax.dynamic_slice_in_dim(attention, shard_idx * out_rows, out_rows, axis=1)
        partial_out = jnp.dot(attn_mine, w_out, preferred_element_type=jnp.float32)
        attn_out = lax.psum(partial_out, 'sp').astype(jnp.bfloat16)
        return attn_out, k_next, v_next

    return jax.shard_map(local_step, mesh=mesh, in_specs=(row_spec, P(), P(), P(), P('sp', None), cache_spec, cache_spec, len_spec, len_spec), out_specs=(row_spec, cache_spec, cache_spec), check_vma=False)
```

profile of v0, /device:TPU:97, one launch (start us, length us, event | category | flops | bytes accessed | tf_op | source)
XLA Modules:
  0.0 168.8 jit_solution(5719332498521333018)
XLA Ops:
  7.2 0.0 copy-start
  7.2 0.1 all-reduce.2.cloned.1.call-start
  7.3 0.7 copy-done
  8.0 7.3 %convolution_convert_fusion.2 = bf16[8,2048]{1,0:T(8,128)(2,1)S(1)} fusion(bf16[8,3584]{1,0:T(8,128)(2,1)S(1)} %copy-done, bf16[3584,2048]{1,0:T(8,128)(2,1)} %param.11), kind=kOutput, calls=%fused_computation.8 | convolution fusion | flops 117456896 | bytes 14770176 | tf_op jit(solution)/shard_map/dot_general | solution.py:21
  15.3 2.0 %copy-done.2 = bf16[3584,2048]{1,0:T(8,128)(2,1)S(1)} copy-done((bf16[3584,2048]{1,0:T(8,128)(2,1)S(1)}, bf16[3584,2048]{1,0:T(8,128)(2,1)}, u32[]{:S(2)}) %copy-start.2) | copy-done | bytes 14680088
  17.4 2.0 %convolution_convert_fusion.1 = bf16[8,2048]{1,0:T(8,128)(2,1)S(1)} fusion(bf16[8,3584]{1,0:T(8,128)(2,1)S(1)} %copy-done, bf16[3584,2048]{1,0:T(8,128)(2,1)S(1)} %copy-done.2), kind=kOutput, calls=%fused_computation.7 | convolution fusion | flops 117456896 | bytes 14770176 | tf_op jit(solution)/shard_map/dot_general | solution.py:22
  19.4 11.8 %convolution_convert_fusion = bf16[8,4096]{1,0:T(8,128)(2,1)S(1)} fusion(bf16[8,3584]{1,0:T(8,128)(2,1)S(1)} %copy-done, bf16[3584,4096]{1,0:T(8,128)(2,1)} %param.10), kind=kOutput, calls=%fused_computation.6 | convolution fusion | flops 234913792 | bytes 29483008 | tf_op jit(solution)/shard_map/dot_general | solution.py:19
  31.3 0.1 broadcast_compare_fusion.1
  31.4 0.4 slice-done.3
  31.8 7.3 %broadcast_select_fusion = (bf16[8,256,8,256]{3,2,1,0:T(8,128)(2,1)}, bf16[8,256,8,256]{3,2,1,0:T(8,128)(2,1)S(1)}) fusion(bf16[8,256,8,256]{3,2,1,0:T(8,128)(2,1)S(1)} %bitcast.15, pred[8,256]{1,0:T(8,128)(4,1)S(1)} %get-tuple-element.8, bf16[8,8,256]{2,1,0:T(8,128)(2,1)S(1)} %copy.25, bf16[8,256,8,256]{3,2,1,0:T(8,128)(2,1)S(1)} %bitcast.17, ...), kind=kLoop, calls=%fused_computation.4 | loop fusion | flops 8388608 | bytes 33622016 | tf_op jit(solution)/shard_map/jit(_where)/select_n | solution.py:26
  39.1 3.4 %copy-done.3 = bf16[8,256,8,256]{3,2,1,0:T(8,128)(2,1)} copy-done((bf16[8,256,8,256]{3,2,1,0:T(8,128)(2,1)}, bf16[8,256,8,256]{3,2,1,0:T(8,128)(2,1)S(1)}, u32[]{:S(2)}) %copy-start.3) | copy-done | bytes 8388632
  42.5 2.3 %fusion.22 = (f32[8,8,2]{2,1,0:T(8,128)S(1)}, f32[8,8,2,256]{3,2,1,0:T(2,128)S(1)}) fusion(bf16[8,256,8,256]{3,2,1,0:T(8,128)(2,1)S(1)} %get-tuple-element.6, bf16[8,8,2,256]{3,0,2,1:T(8,128)(2,1)S(1)} %bitcast.21, pred[8,256]{1,0:T(8,128)(4,1)S(1)} %get-tuple-element.7), kind=kOutput, calls=%fused_computation.29 | convolution fusion | flops 16875392 | bytes 8587776 | tf_op jit(solution)/shard_map/bkgd,bskd->bkgs/dot_general | solution.py:27
  44.9 24.1 %pmax.7 = f32[8,8,2]{2,1,0:T(8,128)S(1)} all-reduce(f32[8,8,2]{2,1,0:T(8,128)S(1)} %broadcast_maximum_fusion), channel_id=1, replica_groups=mesh['rep'=1,'dp'=4,'sp'=8] {'sp'}, use_global_device_ids=true, to_apply=%region_1.2 | all-reduce | flops 128 | bytes 1024 | tf_op jit(solution)/shard_map/pmax | solution.py:34
  69.0 0.3 fusion.14
  69.3 0.5 copy.28
  69.8 4.7 %fusion.7 = f32[8,8,2,256]{3,2,1,0:T(2,128)S(1)} fusion(bf16[8,256,8,256]{3,2,1,0:T(8,128)(2,1)} %get-tuple-element.5, f32[8,8,2,256]{3,2,1,0:T(2,128)S(1)} %get-tuple-element.10, f32[8,8,2]{2,1,0:T(8,128)S(1)} %get-tuple-element.4, f32[8,8,2]{2,1,0:T(8,128)S(1)} %broadcast_maximum_fusion), kind=kOutput, calls=%fused_computation.10 | convolution fusion | flops 16875520 | bytes 8651776 | tf_op jit(solution)/shard_map/bkgs,bskd->bkgd/dot_general | solution.py:33
  74.5 0.8 pad_maximum_fusion
  75.3 0.1 all-reduce.2.cloned.1.call-update
  75.4 56.2 %all-reduce.2.cloned.1.call-done = f32[8,8,2,257]{3,2,1,0:T(2,128)} async-done(((f32[8,8,2,257]{3,2,1,0:T(2,128)}), f32[8,8,2,257]{3,2,1,0:T(2,128)}) %all-reduce.2.cloned.1.call-update) | async-done | bytes 131600 | tf_op jit(solution)/shard_map/psum | solution.py:37
  131.5 0.8 slice.9
  132.4 0.5 copy.33
  132.9 1.0 fusion.13
  134.0 2.6 %fusion.19 = f32[8,3584]{1,0:T(8,128)S(1)} fusion(bf16[512,3584]{1,0:T(8,128)(2,1)} %param.13, bf16[8,4096]{1,0:T(8,128)(2,1)S(1)} %reshape.76, s32[]{:T(128)S(6)} %select_n.17), kind=kOutput, calls=%fused_computation.23 | convolution fusion | flops 29360128 | bytes 3792900 | tf_op jit(solution)/shard_map/dot_general | solution.py:42
  136.6 25.3 %psum.15 = bf16[8,3584]{1,0:T(8,128)(2,1)} all-reduce(f32[8,3584]{1,0:T(8,128)S(1)} %fusion.19), channel_id=1, replica_groups=mesh['rep'=1,'dp'=4,'sp'=8] {'sp'}, use_global_device_ids=true, to_apply=%region_4.5 | all-reduce | flops 28672 | bytes 172032 | tf_op jit(solution)/shard_map/psum | solution.py:43
  (23 shorter events, 0.1 us)
Async XLA Ops:
  7.2 0.8 copy-start
  7.2 124.4 %all-reduce.2.cloned.1.call-start = ((), (), s32[]{:S(2)}) async-start(), calls=%async_computation | async-start | bytes 393216 | tf_op jit(solution)/shard_map/psum | solution.py:37
  8.0 9.3 %copy-start.2 = (bf16[3584,2048]{1,0:T(8,128)(2,1)S(1)}, bf16[3584,2048]{1,0:T(8,128)(2,1)}, u32[]{:S(2)}) copy-start(bf16[3584,2048]{1,0:T(8,128)(2,1)} %param.12) | copy-start | bytes 44040196
  17.4 14.0 %slice-start = ((s8[8388608]{0:T(1024)(128)(4,1)}), s8[4194304]{0:T(1024)(128)(4,1)S(1)}, s32[]{:S(2)}) async-start(s8[8388608]{0:T(1024)(128)(4,1)} %bitcast.14), calls=%async_computation.1 | async-start | bytes 8388608
  17.4 14.0 %slice-start.2 = ((s8[8388608]{0:T(1024)(128)(4,1)}), s8[4194304]{0:T(1024)(128)(4,1)S(1)}, s32[]{:S(2)}) async-start(s8[8388608]{0:T(1024)(128)(4,1)} %bitcast.16), calls=%async_computation.3 | async-start | bytes 8388608
  19.4 11.9 %copy-start.4 = (s32[8]{0:T(128)S(1)}, s32[8]{0:T(128)}, u32[]{:S(2)}) copy-start(s32[8]{0:T(128)} %param.17) | copy-start | bytes 100
  19.4 11.9 %copy-start.5 = (s32[8]{0:T(128)S(1)}, s32[8]{0:T(128)}, u32[]{:S(2)}) copy-start(s32[8]{0:T(128)} %param.16) | copy-start | bytes 100
  19.4 11.9 %slice-start.1 = ((s8[8388608]{0:T(1024)(128)(4,1)}), s8[4194304]{0:T(1024)(128)(4,1)S(1)}, s32[]{:S(2)}) async-start(s8[8388608]{0:T(1024)(128)(4,1)} %bitcast.14), calls=%async_computation.2 | async-start | bytes 8388608
  19.4 12.4 %slice-start.3 = ((s8[8388608]{0:T(1024)(128)(4,1)}), s8[4194304]{0:T(1024)(128)(4,1)S(1)}, s32[]{:S(2)}) async-start(s8[8388608]{0:T(1024)(128)(4,1)} %bitcast.16), calls=%async_computation.4 | async-start | bytes 8388608
  39.1 3.4 %copy-start.3 = (bf16[8,256,8,256]{3,2,1,0:T(8,128)(2,1)}, bf16[8,256,8,256]{3,2,1,0:T(8,128)(2,1)S(1)}, u32[]{:S(2)}) copy-start(bf16[8,256,8,256]{3,2,1,0:T(8,128)(2,1)S(1)} %get-tuple-element.6) | copy-start | bytes 25165828
  42.5 119.4 %copy-start.1 = (bf16[8,3584]{1,0:T(8,128)(2,1)S(1)}, bf16[8,3584]{1,0:T(8,128)(2,1)}, u32[]{:S(2)}) copy-start(bf16[8,3584]{1,0:T(8,128)(2,1)} %param.9) | copy-start | bytes 172036
Sparse Core Ops, SparseCore 0:
  75.5 56.0 all-reduce.1
where the time goes:
time: 171 us; the launch traced here: 169 us
  waiting for transfers between devices  56.3 us (33%)
  blocking collectives  49.4 us (29%)
  matrix products  30.8 us (18%)
  between operations  14.2 us (8%)
  other arithmetic  9.54 us (6%)
  local copies, waits for them, and re-layouts  8.52 us (5%)
    psum x1, waiting for transfers between devices, local_step(): packed = lax.psum(packed, 'sp')  56.2 us
    psum x1, blocking collectives, local_step(): attn_out = lax.psum(partial_out, 'sp').astype(jnp.bfloat16)  25.3 us
    pmax x1, blocking collectives, local_step(): global_max = lax.pmax(local_max, 'sp')  24.1 us
    dot_general x1, matrix products, local_step(): jnp.dot(hidden, w_query, preferred_element_type=jnp.float32)  11.8 us
    select_n x1, other arithmetic, local_step(): jnp.where(at_pos, value_new.reshape(num_rows, 1, kv_heads, head_dim), v_c...  7.33 us
    dot_general x1, matrix products, local_step(): jnp.dot(hidden, w_key, preferred_element_type=jnp.float32)  7.32 us
    unnamed x20, local copies, waits for them, and re-layouts  6.63 us
    dot_general x1, matrix products, local_step(): jnp.einsum('bkgs,bskd->bkgd', weights.astype(jnp.bfloat16), v_next, prefe...  4.73 us
  transfers between devices with their start and end apart: 1, of which 1 were waited for; matrix products, arithmetic and copies ran while one was open for 0% of the time, Pallas kernels for 0%

commit v1 on v0

v1 whole, which is shorter than its diff:
```python
import functools

import jax
import jax.numpy as jnp
from jax import lax
from jax.experimental import pallas as pl
from jax.experimental.pallas import tpu as pltpu
from jax.sharding import PartitionSpec as P

F32 = jnp.float32
BF16 = jnp.bfloat16
FLOOR = float(jnp.finfo(jnp.float32).min)
MESH = pl.DeviceIdType.MESH
W_CHUNKS = 4
TILE = 32
MIB = 1 << 20


def _peer(me, off, n):
    return lax.rem(me + off, n)


def _greet(me, n):
    barrier = pltpu.get_barrier_semaphore()
    for off in range(1, n):
        pl.semaphore_signal(barrier, inc=1, device_id={'sp': _peer(me, off, n)}, device_id_type=MESH)
    return barrier


def _exchange(me, n, src, dst, ssem, rsem):
    return [
        pltpu.make_async_remote_copy(
            src_ref=src(_peer(me, off, n)), dst_ref=dst(off), send_sem=ssem.at[off - 1], recv_sem=rsem.at[off - 1],
            device_id={'sp': _peer(me, off, n)}, device_id_type=MESH)
        for off in range(1, n)
    ]


def _rows(i, count):
    return pl.ds(pl.multiple_of(i * count, count), count)


def _project(n, hid_ref, wq_ref, wk_ref, wv_ref, kc_ref, vc_ref,
             all_ref, k_ref, v_ref,
             hid, wqb, wkb, wvb, mine, got,
             hsem, wsem, ksem, vsem, s1, r1):
    me = lax.axis_index('sp')
    rows = hid.shape[0]
    depth, qw = wqb.shape
    dim = wkb.shape[1]
    ck = depth // W_CHUNKS
    hcopy = pltpu.make_async_copy(hid_ref, hid, hsem)
    hcopy.start()

    def w_copies(c):
        rs = pl.ds(c * ck, ck)
        return [
            pltpu.make_async_copy(wq_ref.at[rs, _rows(me, qw)], wqb.at[rs], wsem.at[c, 0]),
            pltpu.make_async_copy(wk_ref.at[rs, _rows(me, dim)], wkb.at[rs], wsem.at[c, 1]),
            pltpu.make_async_copy(wv_ref.at[rs, _rows(me, dim)], wvb.at[rs], wsem.at[c, 2]),
        ]

    def kv_copies(b):
        return [
            pltpu.make_async_copy(kc_ref.at[b], k_ref.at[b], ksem.at[b]),
            pltpu.make_async_copy(vc_ref.at[b], v_ref.at[b], vsem.at[b]),
        ]

    for c in range(W_CHUNKS):
        for cp in w_copies(c):
            cp.start()
    barrier = _greet(me, n)
    hcopy.wait()
    acc_q = jnp.zeros((rows, qw), F32)
    acc_k = jnp.zeros((rows, dim), F32)
    acc_v = jnp.zeros((rows, dim), F32)
    for c in range(W_CHUNKS):
        for cp in w_copies(c):
            cp.wait()
        for b in range(c * rows // W_CHUNKS, (c + 1) * rows // W_CHUNKS):
            for cp in kv_copies(b):
                cp.start()
        rs = pl.ds(c * ck, ck)
        h = hid[:, rs]
        acc_q += jnp.dot(h, wqb[rs], preferred_element_type=F32)
        acc_k += jnp.dot(h, wkb[rs], preferred_element_type=F32)
        acc_v += jnp.dot(h, wvb[rs], preferred_element_type=F32)
    mine[:, :qw] = acc_q.astype(BF16)
    mine[:, qw:qw + dim] = acc_k.astype(BF16)
    mine[:, qw + dim:] = acc_v.astype(BF16)
    pl.semaphore_wait(barrier, n - 1)
    x1 = _exchange(me, n, lambda peer: mine, lambda off: got.at[off - 1], s1, r1)
    for cp in x1:
        cp.start()

    def spread(src, value):
        value = value.astype(F32)
        for c in range(value.shape[1] // 128):
            all_ref[c, _rows(src, rows), :] = value[:, c * 128:(c + 1) * 128]

    spread(me, mine[...])
    for off in range(1, n):
        x1[off - 1].wait()
        spread(_peer(me, n - off, n), got[off - 1])
    for b in range(rows):
        for cp in kv_copies(b):
            cp.wait()


def _attend(n, wp_ref, vl_ref, all_ref, ki_ref, vi_ref, k_ref, v_ref, ko_ref, vo_ref, acc_ref, st_ref, ksem, vsem):
    del ki_ref, vi_ref
    me = lax.axis_index('sp')
    rows, seq, heads, dim = ko_ref.shape
    width = seq * heads
    ntile = seq // TILE
    w = TILE * heads
    scale = dim ** -0.5
    lane = lax.broadcasted_iota(jnp.int32, (heads, 128), 1)
    blocks = dim // 128

    def new_rows(b, first):
        return jnp.concatenate([all_ref[first + c, pl.ds(b, n, stride=rows), :] for c in range(blocks)], axis=1)

    def copies(b):
        return [
            pltpu.make_async_copy(k_ref.at[b], ko_ref.at[b], ksem.at[b]),
            pltpu.make_async_copy(v_ref.at[b], vo_ref.at[b], vsem.at[b]),
        ]

    for b in range(rows):
        at = wp_ref[b] - me * seq

        @pl.when((at >= 0) & (at < seq))
        def _():
            k_ref[b, at] = new_rows(b, 2 * blocks).astype(BF16)
            v_ref[b, at] = new_rows(b, 3 * blocks).astype(BF16)

    for b in range(rows):
        for cp in copies(b):
            cp.start()
    col = lax.broadcasted_iota(jnp.int32, (2 * heads, width), 1)
    row = lax.broadcasted_iota(jnp.int32, (2 * heads, width), 0)
    same = (col % heads) == (row % heads)
    colpos = col // heads

    def step(b, carry):
        q = jnp.concatenate([new_rows(b, 0), new_rows(b, blocks)], axis=0).astype(BF16)
        vl = vl_ref[b] - me * seq
        scores = []
        for t in range(ntile):
            kt = k_ref[b, pl.ds(t * TILE, TILE)].reshape(w, dim)
            scores.append(lax.dot_general(q, kt, (((1,), (1,)), ((), ())), preferred_element_type=F32))
        s = jnp.concatenate(scores, axis=1) * scale
        s = jnp.where(same & (colpos < vl), s, -jnp.inf)
        m = jnp.maximum(jnp.max(s, axis=-1, keepdims=True), FLOOR)
        p = jnp.exp(s - m)
        l = jnp.sum(p, axis=-1, keepdims=True)
        pb = p.astype(BF16)
        acc = jnp.zeros((2 * heads, dim), F32)
        for t in range(ntile):
            vt = v_ref[b, pl.ds(t * TILE, TILE)].reshape(w, dim)
            acc += jnp.dot(pb[:, t * w:(t + 1) * w], vt, preferred_element_type=F32)
        for c in range(blocks):
            piece = acc[:, c * 128:(c + 1) * 128]
            acc_ref[c, pl.ds(b, heads, stride=2 * rows), :] = piece[:heads]
            acc_ref[c, pl.ds(b + rows, heads, stride=2 * rows), :] = piece[heads:]
        st = jnp.where(lane == 0, m[:heads], jnp.where(lane == 1, l[:heads], jnp.where(lane == 2, m[heads:], l[heads:])))
        st_ref[pl.ds(b, heads, stride=rows), :] = st
        return carry

    lax.fori_loop(0, rows, step, 0)
    for b in range(rows):
        for cp in copies(b):
            cp.wait()


def _finish(n, sacc, st_ref, wo_ref, out_ref, w_ref, racc, rst, part, recv, red, gath,
            wsem, s2, r2, s3, r3, s4, r4, s5, r5):
    me = lax.axis_index('sp')
    rows, model = out_ref.shape
    blocks = sacc.shape[0]
    cols = part.shape[1] // n
    wcopy = pltpu.make_async_copy(wo_ref, w_ref, wsem)
    wcopy.start()
    barrier = _greet(me, n)
    pl.semaphore_wait(barrier, n - 1)
    x2 = _exchange(me, n, lambda peer: sacc.at[:, _rows(peer, 2 * rows)], lambda off: racc.at[off - 1], s2, r2)
    x3 = _exchange(me, n, lambda peer: st_ref.at[_rows(peer, rows)], lambda off: rst.at[off - 1], s3, r3)
    for a, b in zip(x2, x3):
        b.start()
        a.start()
    racc[n - 1] = sacc[:, _rows(me, 2 * rows), :]
    sts = [st_ref[_rows(me, rows), :]]
    for off in range(1, n):
        x3[off - 1].wait()
        sts.append(rst[off - 1])
    order = [n - 1] + list(range(n - 1))
    scales, totals = [], []
    for j in range(2):
        ms = [st[:, 2 * j:2 * j + 1] for st in sts]
        top = functools.reduce(jnp.maximum, ms)
        scales.append([jnp.exp(m - top) for m in ms])
        totals.append(functools.reduce(jnp.add, [st[:, 2 * j + 1:2 * j + 2] * e for st, e in zip(sts, scales[j])]))
    for cp in x2:
        cp.wait()
    pieces = []
    for j in range(2):
        for c in range(blocks):
            num = functools.reduce(jnp.add, [racc[i, c, j * rows:(j + 1) * rows, :] * e for i, e in zip(order, scales[j])])
            pieces.append((num / totals[j]).astype(BF16))
    o = jnp.concatenate(pieces, axis=1)
    wcopy.wait()
    part[:, :model] = jnp.dot(o, w_ref[...], preferred_element_type=F32)
    part[:, model:] = jnp.zeros((rows, part.shape[1] - model), F32)
    rs = _exchange(me, n, lambda peer: part.at[:, _rows(peer, cols)], lambda off: recv.at[off - 1], s4, r4)
    for cp in rs:
        cp.start()
    total = part[:, _rows(me, cols)]
    for off in range(1, n):
        rs[off - 1].wait()
        total += recv[off - 1]
    red[...] = total.astype(BF16)
    ag = _exchange(me, n, lambda peer: red, lambda off: gath.at[:, _rows(me, cols)], s5, r5)
    for cp in ag:
        cp.start()
    for cp in ag:
        cp.wait()
    gath[:, _rows(me, cols)] = red[...]
    out_ref[...] = gath[:, :model]


def solution(mesh):
    row_spec = P(('rep', 'dp'), None)
    cache_spec = P(('rep', 'dp'), 'sp', None, None)
    len_spec = P(('rep', 'dp'))
    n = mesh.shape['sp']
    vmem = pl.BlockSpec(memory_space=pltpu.VMEM)
    smem = pl.BlockSpec(memory_space=pltpu.SMEM)
    hbm = pl.BlockSpec(memory_space=pltpu.HBM)
    dma = pltpu.SemaphoreType.DMA

    def in_hbm(x):
        return pltpu.with_memory_space_constraint(x, pltpu.HBM)

    def local_step(hidden, w_query, w_key, w_value, w_out, k_cache, v_cache, write_pos, valid_len):
        rows, seq, heads, dim = k_cache.shape
        depth = hidden.shape[1]
        model = w_out.shape[1]
        qw = w_query.shape[1] // n
        lw = qw + 2 * dim
        blocks = dim // 128
        cache = pltpu.VMEM(k_cache.shape, BF16)
        proj, k_here, v_here = pl.pallas_call(
            functools.partial(_project, n),
            out_shape=(pltpu.VMEM((lw // 128, n * rows, 128), F32), cache, cache),
            in_specs=[hbm] * 6,
            out_specs=(vmem,) * 3,
            scratch_shapes=[
                pltpu.VMEM((rows, depth), BF16),
                pltpu.VMEM((depth, qw), BF16),
                pltpu.VMEM((depth, dim), BF16),
                pltpu.VMEM((depth, dim), BF16),
                pltpu.VMEM((rows, lw), BF16),
                pltpu.VMEM((n - 1, rows, lw), BF16),
                dma, dma((W_CHUNKS, 3)), dma((rows,)), dma((rows,)), dma((n - 1,)), dma((n - 1,)),
            ],
            compiler_params=pltpu.CompilerParams(collective_id=0, has_side_effects=True, vmem_limit_bytes=12 * MIB),
            cost_estimate=pl.CostEstimate(flops=10_000_000_000, bytes_accessed=28 * MIB, transcendentals=0),
            name='project',
        )(*[in_hbm(x) for x in (hidden, w_query, w_key, w_value, k_cache, v_cache)])
        _, _, k_next, v_next, acc, st = pl.pallas_call(
            functools.partial(_attend, n),
            out_shape=(
                cache, cache,
                jax.ShapeDtypeStruct(k_cache.shape, BF16),
                jax.ShapeDtypeStruct(v_cache.shape, BF16),
                pltpu.VMEM((blocks, heads * 2 * rows, 128), F32),
                pltpu.VMEM((heads * rows, 128), F32),
            ),
            in_specs=[smem, smem, vmem, vmem, vmem],
            out_specs=(vmem, vmem, hbm, hbm, vmem, vmem),
            scratch_shapes=[dma((rows,)), dma((rows,))],
            input_output_aliases={3: 0, 4: 1},
            compiler_params=pltpu.CompilerParams(vmem_limit_bytes=8 * MIB),
            cost_estimate=pl.CostEstimate(flops=5_000_000_000, bytes_accessed=16 * MIB, transcendentals=0),
            name='attend',
        )(write_pos, valid_len, proj, k_here, v_here)
        padded = -(-model // (128 * n)) * 128 * n
        attn = pl.pallas_call(
            functools.partial(_finish, n),
            out_shape=jax.ShapeDtypeStruct((rows, model), BF16),
            in_specs=[vmem, vmem, hbm],
            out_specs=vmem,
            scratch_shapes=[
                pltpu.VMEM(w_out.shape, BF16),
                pltpu.VMEM((n, blocks, 2 * rows, 128), F32),
                pltpu.VMEM((n - 1, rows, 128), F32),
                pltpu.VMEM((rows, padded), F32),
                pltpu.VMEM((n - 1, rows, padded // n), F32),
                pltpu.VMEM((rows, padded // n), BF16),
                pltpu.VMEM((rows, padded), BF16),
                dma,
            ] + [dma((n - 1,))] * 8,
            compiler_params=pltpu.CompilerParams(collective_id=1, has_side_effects=True, vmem_limit_bytes=8 * MIB),
            cost_estimate=pl.CostEstimate(flops=20_000_000_000, bytes_accessed=4 * MIB, transcendentals=0),
            name='finish',
        )(acc, st, in_hbm(w_out))
        return attn, k_next, v_next

    return jax.shard_map(
        local_step, mesh=mesh,
        in_specs=(row_spec, P(), P(), P(), P('sp', None), cache_spec, cache_spec, len_spec, len_spec),
        out_specs=(row_spec, cache_spec, cache_spec), check_vma=False)
```

time: 171 us -> 36.5 us (0.21); the launches traced: 169 us -> 36.4 us
  waiting for transfers between devices: 56.3 us -> 0 us
  blocking collectives: 49.4 us -> 0 us
  Pallas kernels: 0 us -> 35.1 us
  matrix products: 30.8 us -> 0 us
  between operations: 14.2 us -> 0.69 us
  other arithmetic: 9.54 us -> 0 us
  local copies, waits for them, and re-layouts: 8.52 us -> 0.63 us
    psum x1 -> x0, waiting for transfers between devices: 56.2 us -> none  [local_step(): packed = lax.psum(packed, 'sp')]
    pallas_call x0 -> x3, Pallas kernels: none -> 35.1 us  [the longest x1 15.6 us: local_step(): pl.pallas_call(functools.partial(_finish, n), out_shape=jax.ShapeDtypeStr...]
    dot_general x6 -> x0, matrix products: 30.8 us -> none  [the longest x1 11.8 us: local_step(): jnp.dot(hidden, w_query, preferred_element_type=jnp.float32)]
    psum x1 -> x0, blocking collectives: 25.3 us -> none  [local_step(): attn_out = lax.psum(partial_out, 'sp').astype(jnp.bfloat16)]
    pmax x1 -> x0, blocking collectives: 24.1 us -> none  [local_step(): global_max = lax.pmax(local_max, 'sp')]
    select_n x1 -> x0, other arithmetic: 7.33 us -> none  [local_step(): jnp.where(at_pos, value_new.reshape(num_rows, 1, kv_heads, head_dim), v_c...]
    unnamed x20 -> x5, local copies, waits for them, and re-layouts: 6.63 us -> 0.63 us
  transfers between devices with their start and end apart: 1 -> 0, of which waited for: 1 -> 0; matrix products, arithmetic and copies ran while one was open for 0% -> 0% of each run, Pallas kernels for 0% -> 0%
where the time goes in v1:
time: 36.5 us; the launch traced here: 36.4 us
  Pallas kernels  35.1 us (96%)
  between operations  0.69 us (2%)
  local copies, waits for them, and re-layouts  0.63 us (2%)
    pallas_call x1, Pallas kernels, local_step(): pl.pallas_call(functools.partial(_finish, n), out_shape=jax.ShapeDtypeStr...  15.6 us
    pallas_call x1, Pallas kernels, local_step(): pl.pallas_call(functools.partial(_project, n), out_shape=(pltpu.VMEM((lw...  11 us
    pallas_call x1, Pallas kernels, local_step(): pl.pallas_call(functools.partial(_attend, n), out_shape=(cache, cache, ja...  8.58 us

profile of v1, /device:TPU:97, one launch (start us, length us, event | category | flops | bytes accessed | tf_op | source)
XLA Modules:
  0.0 36.4 jit_solution(8377865708958579288)
XLA Ops:
  0.6 0.0 copy-start.1
  0.6 0.0 copy-start
  0.7 11.0 %project.1 = (f32[8,64,128]{2,1,0:T(8,128)S(1)}, bf16[8,256,8,256]{3,2,1,0:T(8,128)(2,1)S(1)}, bf16[8,256,8,256]{3,2,1,0:T(8,128)(2,1)S(1)}) custom-call(bf16[8,3584]{1,0:T(8,128)(2,1)} %hid_ref.1, bf16[3584,4096]{1,0:T(8,128)(2,1)} %wq_ref.1, bf16[3584,2048]{1,0:T(8,128)(2,1)} %wk_ref.1, bf16[3584,2048]{1,0:T(8,128)(2,1)} %wv_ref.1, ...), custom_call_target="tpu_custom_call" | custom-call | flops 10000000000 | bytes 29360128 | tf_op jit(solution)/shard_map/project/pallas_call | solution.py:253
  11.6 0.0 copy-done.1
  11.6 0.0 copy-done
  11.7 8.6 %attend.1 = (bf16[8,256,8,256]{3,2,1,0:T(8,128)(2,1)S(1)}, bf16[8,256,8,256]{3,2,1,0:T(8,128)(2,1)S(1)}, bf16[8,256,8,256]{3,2,1,0:T(8,128)(2,1)}, bf16[8,256,8,...) custom-call(s32[8]{0:T(128)S(1)} %copy-done, ...), custom_call_target="tpu_custom_call", output_to_operand_aliasing={{0}: (3, {}), {1}: (4, {})} | custom-call | flops 5000000000 | bytes 16777216 | tf_op jit(solution)/shard_map/attend/pallas_call | solution.py:271
  20.2 15.6 %finish.1 = bf16[8,3584]{1,0:T(8,128)(2,1)S(1)} custom-call(f32[2,128,128]{2,1,0:T(8,128)S(1)} %get-tuple-element.13.sacc, f32[64,128]{1,0:T(8,128)S(1)} %get-tuple-element.14.st_ref, bf16[512,3584]{1,0:T(8,128)(2,1)} %wo_ref.1), custom_call_target="tpu_custom_call" | custom-call | flops 20000000000 | bytes 4194304 | tf_op jit(solution)/shard_map/finish/pallas_call | solution.py:289
  35.8 0.6 %copy.17 = bf16[8,3584]{1,0:T(8,128)(2,1)} copy(bf16[8,3584]{1,0:T(8,128)(2,1)S(1)} %finish.1) | data formatting | bytes 114688
Async XLA Ops:
  0.6 11.0 %copy-start.1 = (s32[8]{0:T(128)S(1)}, s32[8]{0:T(128)}, u32[]{:S(2)}) copy-start(s32[8]{0:T(128)} %vl_ref.1) | copy-start | bytes 100
  0.6 11.0 %copy-start = (s32[8]{0:T(128)S(1)}, s32[8]{0:T(128)}, u32[]{:S(2)}) copy-start(s32[8]{0:T(128)} %wp_ref.1) | copy-start | bytes 100

commit v2 on v0

v2 whole, which is shorter than its diff:
```python
import functools

import jax
import jax.numpy as jnp
from jax import lax
from jax.experimental import pallas as pl
from jax.experimental.pallas import tpu as pltpu
from jax.sharding import PartitionSpec as P

F32 = jnp.float32
BF16 = jnp.bfloat16
FLOOR = float(jnp.finfo(jnp.float32).min)
MESH = pl.DeviceIdType.MESH
W_PARTS = (5, 4, 3, 2)
K_AFTER = (0, 0, 4, 16, 16)
EARLY = 5
TILE = 32
LAG = 2
MIB = 1 << 20


def _peer(me, off, n):
    return lax.rem(me + off, n)


def _greet(me, n):
    barrier = pltpu.get_barrier_semaphore()
    for off in range(1, n):
        pl.semaphore_signal(barrier, inc=1, device_id={'sp': _peer(me, off, n)}, device_id_type=MESH)
    return barrier


def _exchange(me, n, src, dst, ssem, rsem):
    def copy(off):
        peer = _peer(me, off, n)
        return pltpu.make_async_remote_copy(
            src_ref=src(peer), dst_ref=dst(off), send_sem=ssem.at[off - 1], recv_sem=rsem.at[off - 1],
            device_id={'sp': peer}, device_id_type=MESH)

    copies = [copy(off) for off in range(1, n)]
    for i in sorted(range(n - 1), key=lambda i: abs(i + 1 - n // 2)):
        copies[i].start()
    return copies


def _positions(heads, width, never):
    col = lax.broadcasted_iota(jnp.int32, (2 * heads, width), 1)
    row = lax.broadcasted_iota(jnp.int32, (2 * heads, width), 0)
    return jnp.where((col % heads) == (row % heads), col // heads, never)


def _rows(i, count):
    return pl.ds(pl.multiple_of(i * count, count), count)


def _project(n, hid_ref, wq_ref, wk_ref, wv_ref, kc_ref, vc_ref, wp_ref, vl_ref,
             s_ref, q_ref, end_ref, hit_ref, kn_ref, vn_ref, k_ref, v_ref,
             hid, wqb, wkb, wvb, acc, mine, got, full, wp, vl,
             hsem, wsem, ksem, vsem, psem, s1, r1):
    me = lax.axis_index('sp')
    rows, seq, heads, dim = k_ref.shape
    depth, qw = wqb.shape
    blocks = dim // 128
    w = TILE * heads
    small = [
        pltpu.make_async_copy(hid_ref, hid, hsem),
        pltpu.make_async_copy(wp_ref, wp, psem.at[0]),
        pltpu.make_async_copy(vl_ref, vl, psem.at[1]),
    ]
    for cp in small:
        cp.start()
    edges = [0]
    for part in W_PARTS:
        edges.append(edges[-1] + depth // dim * part // sum(W_PARTS) * dim)
    chunks = len(W_PARTS)

    def w_copies(c):
        rs = pl.ds(edges[c], edges[c + 1] - edges[c])
        return [
            pltpu.make_async_copy(wq_ref.at[rs, _rows(me, qw)], wqb.at[rs], wsem.at[c, 0]),
            pltpu.make_async_copy(wk_ref.at[rs, _rows(me, dim)], wkb.at[rs], wsem.at[c, 1]),
            pltpu.make_async_copy(wv_ref.at[rs, _rows(me, dim)], wvb.at[rs], wsem.at[c, 2]),
        ]

    k_copies = [pltpu.make_async_copy(kc_ref.at[b], k_ref.at[b], ksem.at[b]) for b in range(rows)]
    v_copies = [pltpu.make_async_copy(vc_ref.at[b], v_ref.at[b], vsem.at[b]) for b in range(rows)]
    queue = k_copies + v_copies
    for c in range(chunks):
        for cp in w_copies(c):
            cp.start()
    barrier = _greet(me, n)
    for cp in small:
        cp.wait()

    for c in range(chunks):
        for cp in w_copies(c):
            cp.wait()
        for cp in queue[len(queue) * K_AFTER[c] // 16:len(queue) * K_AFTER[c + 1] // 16]:
            cp.start()

        @pl.when(me >= 0)
        def _():
            ks = pl.ds(edges[c], edges[c + 1] - edges[c])
            parts = [jnp.dot(hid[:, ks], ref[ks, :], preferred_element_type=F32) for ref in (wqb, wkb, wvb)]
            total = jnp.concatenate(parts, axis=1)
            acc[...] = total if c == 0 else acc[...] + total

    mine[...] = acc[...].astype(BF16)
    pl.semaphore_wait(barrier, n - 1)
    x1 = _exchange(me, n, lambda peer: mine, lambda off: got.at[off - 1], s1, r1)

    def spread(src, value):
        value = value.astype(F32)
        for c in range(value.shape[1] // 128):
            full[c, _rows(src, rows), :] = value[:, c * 128:(c + 1) * 128]

    pos = lax.broadcasted_iota(jnp.int32, (1, seq), 1) + me * seq
    for b in range(rows):
        hit_ref[b:b + 1, :] = jnp.where(pos == wp[b], 1, 0)
    spread(me, mine[...])
    for off in range(1, n):
        x1[off - 1].wait()
        spread(_peer(me, n - off, n), got[off - 1])

    def of_row(b, first):
        return jnp.concatenate([full[first * blocks + c, pl.ds(b, n, stride=rows), :] for c in range(blocks)], axis=1)

    colpos = _positions(heads, w, 2 * seq * n)
    ntile = seq // TILE
    scale = dim ** -0.5

    for b in range(rows):
        q = jnp.concatenate([of_row(b, 0), of_row(b, 1)], axis=0).astype(BF16)
        kn = of_row(b, 2).astype(BF16)
        end = vl[b] - me * seq
        at = wp[b] - me * seq
        q_ref[b] = q
        kn_ref[b] = kn
        vn_ref[b] = of_row(b, 3).astype(BF16)
        end_ref[b:b + 1, :] = jnp.full((1, w), end, jnp.int32)
        if b >= EARLY:
            continue
        k_copies[b].wait()

        def times(kt):
            return lax.dot_general(q, kt, (((1,), (1,)), ((), ())), preferred_element_type=F32)

        fresh = times(jnp.concatenate([kn[None]] * TILE, axis=0).reshape(w, dim))
        for t in range(ntile):
            s = jnp.where(colpos == at - t * TILE, fresh, times(k_ref[b, pl.ds(t * TILE, TILE)].reshape(w, dim))) * scale
            s_ref[b, :, t * w:(t + 1) * w] = jnp.where(colpos < end - t * TILE, s, -jnp.inf)

    for cp in k_copies[EARLY:]:
        cp.wait()
    for cp in v_copies:
        cp.wait()


def _attend(n, s_ref, q_ref, end_ref, k_ref, v_ref, wo_ref, out_ref, w_ref, p_ref, xs, xr, part, recv, red, gath,
            wsem, s2, r2, s4, r4, s5, r5):
    me = lax.axis_index('sp')
    rows, seq, heads, dim = v_ref.shape
    model = out_ref.shape[1]
    cols = part.shape[1] // n
    blocks = dim // 128
    ntile = seq // TILE
    w = TILE * heads
    span = xs.shape[0] // heads
    wcopy = pltpu.make_async_copy(wo_ref, w_ref, wsem)
    wcopy.start()
    barrier = _greet(me, n)
    lane = lax.broadcasted_iota(jnp.int32, (heads, 128), 1)
    colpos = _positions(heads, w, 2 * seq * n)
    scale = dim ** -0.5

    def score(b):
        return [lax.dot_general(q_ref[b], k_ref[b, pl.ds(t * TILE, TILE)].reshape(w, dim), (((1,), (1,)), ((), ())),
                                preferred_element_type=F32) for t in range(ntile)]

    def soften(b, ss):
        if ss is None:
            ss = [s_ref[b, :, t * w:(t + 1) * w] for t in range(ntile)]
        else:
            end = end_ref[b:b + 1, :]
            ss = [jnp.where(colpos < end - t * TILE, s * scale, -jnp.inf) for t, s in enumerate(ss)]
        m = jnp.max(functools.reduce(jnp.maximum, ss), axis=-1, keepdims=True)
        m = jnp.maximum(m, FLOOR)
        ps = [jnp.exp(s - m) for s in ss]
        l = jnp.sum(functools.reduce(jnp.add, ps), axis=-1, keepdims=True)
        for t in range(ntile):
            p_ref[b, :, t * w:(t + 1) * w] = ps[t].astype(BF16)
        st = jnp.where(lane == 0, m[:heads], jnp.where(lane == 1, l[:heads], jnp.where(lane == 2, m[heads:], l[heads:])))
        xs[pl.ds(blocks * 2 * rows + b, heads, stride=span), :] = st

    def values(b):
        acc = functools.reduce(jnp.add, [
            functools.reduce(jnp.add, [
                jnp.dot(p_ref[b, :, t * w:(t + 1) * w], v_ref[b, pl.ds(t * TILE, TILE)].reshape(w, dim),
                        preferred_element_type=F32) for t in range(first, ntile, 2)]) for first in range(2)])
        for c in range(blocks):
            piece = acc[:, c * 128:(c + 1) * 128]
            xs[pl.ds(c * 2 * rows + b, heads, stride=span), :] = piece[:heads]
            xs[pl.ds(c * 2 * rows + rows + b, heads, stride=span), :] = piece[heads:]

    for i in range(rows + LAG):
        if i < rows:
            soften(i, score(i) if i >= EARLY else None)
        if i >= LAG:
            values(i - LAG)
    pl.semaphore_wait(barrier, n - 1)
    x2 = _exchange(me, n, lambda peer: xs.at[_rows(peer, span)], lambda off: xr.at[off - 1], s2, r2)
    xr[n - 1] = xs[_rows(me, span), :]
    for cp in x2:
        cp.wait()
    base = blocks * 2 * rows
    pieces = []
    sts = [xr[i, base:base + rows, :] for i in range(n)]
    for j in range(2):
        ms = [st[:, 2 * j:2 * j + 1] for st in sts]
        top = functools.reduce(jnp.maximum, ms)
        es = [jnp.exp(m - top) for m in ms]
        total = functools.reduce(jnp.add, [st[:, 2 * j + 1:2 * j + 2] * e for st, e in zip(sts, es)])
        for c in range(blocks):
            at = c * 2 * rows + j * rows
            num = functools.reduce(jnp.add, [xr[i, at:at + rows, :] * es[i] for i in range(n)])
            pieces.append((num / total).astype(BF16))
    o = jnp.concatenate(pieces, axis=1)
    wcopy.wait()

    part[:, :model] = jnp.dot(o, w_ref[...], preferred_element_type=F32)
    part[:, model:] = jnp.zeros((rows, part.shape[1] - model), F32)
    rs = _exchange(me, n, lambda peer: part.at[:, _rows(peer, cols)], lambda off: recv.at[off - 1], s4, r4)
    total = part[:, _rows(me, cols)]
    for off in range(1, n):
        rs[off - 1].wait()
        total += recv[off - 1]
    red[...] = total.astype(BF16)
    ag = _exchange(me, n, lambda peer: red, lambda off: gath.at[:, _rows(me, cols)], s5, r5)
    for cp in ag:
        cp.wait()
    gath[:, _rows(me, cols)] = red[...]
    out_ref[...] = gath[:, :model]


def _hand_over(attn_ref, k_ref, v_ref, out_ref):
    del k_ref, v_ref
    out_ref[...] = attn_ref[...]


def solution(mesh):
    row_spec = P(('rep', 'dp'), None)
    cache_spec = P(('rep', 'dp'), 'sp', None, None)
    len_spec = P(('rep', 'dp'))
    n = mesh.shape['sp']
    vmem = pl.BlockSpec(memory_space=pltpu.VMEM)
    hbm = pl.BlockSpec(memory_space=pltpu.HBM)
    dma = pltpu.SemaphoreType.DMA

    def in_hbm(x):
        return pltpu.with_memory_space_constraint(x, pltpu.HBM)

    def local_step(hidden, w_query, w_key, w_value, w_out, k_cache, v_cache, write_pos, valid_len):
        rows, seq, heads, dim = k_cache.shape
        depth = hidden.shape[1]
        model = w_out.shape[1]
        qw = w_query.shape[1] // n
        lw = qw + 2 * dim
        blocks = dim // 128
        cache = pltpu.VMEM(k_cache.shape, BF16)
        new = pltpu.VMEM((rows, heads, dim), BF16)
        scores, query, ends, hit, k_new, v_new, k_here, v_here = pl.pallas_call(
            functools.partial(_project, n),
            out_shape=(
                pltpu.VMEM((EARLY, 2 * heads, seq * heads), F32),
                pltpu.VMEM((rows, 2 * heads, dim), BF16),
                pltpu.VMEM((rows, TILE * heads), jnp.int32),
                pltpu.VMEM((rows, seq), jnp.int32),
                new, new, cache, cache,
            ),
            in_specs=[hbm] * 8,
            out_specs=(vmem,) * 8,
            scratch_shapes=[
                pltpu.VMEM((rows, depth), BF16),
                pltpu.VMEM((depth, qw), BF16),
                pltpu.VMEM((depth, dim), BF16),
                pltpu.VMEM((depth, dim), BF16),
                pltpu.VMEM((rows, lw), F32),
                pltpu.VMEM((rows, lw), BF16),
                pltpu.VMEM((n - 1, rows, lw), BF16),
                pltpu.VMEM((lw // 128, n * rows, 128), F32),
                pltpu.SMEM((rows,), jnp.int32),
                pltpu.SMEM((rows,), jnp.int32),
                dma, dma((len(W_PARTS), 3)), dma((rows,)), dma((rows,)), dma((2,)), dma((n - 1,)), dma((n - 1,)),
            ],
            compiler_params=pltpu.CompilerParams(collective_id=0, has_side_effects=True, vmem_limit_bytes=12 * MIB),
            cost_estimate=pl.CostEstimate(flops=10_000_000_000, bytes_accessed=28 * MIB, transcendentals=0),
            name='project',
        )(*[in_hbm(x) for x in (hidden, w_query, w_key, w_value, k_cache, v_cache, write_pos, valid_len)])
        at_pos = (hit != 0)[:, :, None, None]
        k_next = jnp.where(at_pos, k_new[:, None], k_here)
        v_next = jnp.where(at_pos, v_new[:, None], v_here)
        padded = -(-model // (128 * n)) * 128 * n
        span = 2 * rows * blocks + rows
        attn = pl.pallas_call(
            functools.partial(_attend, n),
            out_shape=jax.ShapeDtypeStruct((rows, model), BF16),
            in_specs=[vmem] * 5 + [hbm],
            out_specs=vmem,
            scratch_shapes=[
                pltpu.VMEM(w_out.shape, BF16),
                pltpu.VMEM((rows, 2 * heads, seq * heads), BF16),
                pltpu.VMEM((heads * span, 128), F32),
                pltpu.VMEM((n, span, 128), F32),
                pltpu.VMEM((rows, padded), F32),
                pltpu.VMEM((n - 1, rows, padded // n), F32),
                pltpu.VMEM((rows, padded // n), BF16),
                pltpu.VMEM((rows, padded), BF16),
                dma,
            ] + [dma((n - 1,))] * 6,
            compiler_params=pltpu.CompilerParams(collective_id=1, has_side_effects=True, vmem_limit_bytes=8 * MIB),
            cost_estimate=pl.CostEstimate(flops=20_000_000_000, bytes_accessed=4 * MIB, transcendentals=0),
            name='attend',
        )(scores, query, ends, k_next, v_next, in_hbm(w_out))
        attn = pl.pallas_call(
            _hand_over,
            out_shape=jax.ShapeDtypeStruct((rows, model), BF16),
            in_specs=[vmem] * 3,
            out_specs=vmem,
            compiler_params=pltpu.CompilerParams(vmem_limit_bytes=1 * MIB),
            name='hand_over',
        )(attn, k_next, v_next)
        return attn, k_next, v_next

    return jax.shard_map(
        local_step, mesh=mesh,
        in_specs=(row_spec, P(), P(), P(), P('sp', None), cache_spec, cache_spec, len_spec, len_spec),
        out_specs=(row_spec, cache_spec, cache_spec), check_vma=False)
```

time: 171 us -> 32.4 us (0.19); the launches traced: 169 us -> 32.4 us
  waiting for transfers between devices: 56.3 us -> 0 us
  blocking collectives: 49.4 us -> 0 us
  matrix products: 30.8 us -> 0 us
  Pallas kernels: 0 us -> 28.8 us
  between operations: 14.2 us -> 0.7 us
  local copies, waits for them, and re-layouts: 8.52 us -> 0.01 us
  other arithmetic: 9.54 us -> 2.88 us
    psum x1 -> x0, waiting for transfers between devices: 56.2 us -> none  [local_step(): packed = lax.psum(packed, 'sp')]
    dot_general x6 -> x0, matrix products: 30.8 us -> none  [the longest x1 11.8 us: local_step(): jnp.dot(hidden, w_query, preferred_element_type=jnp.float32)]
    pallas_call x0 -> x3, Pallas kernels: none -> 28.8 us  [the longest x1 14.8 us: local_step(): pl.pallas_call(functools.partial(_attend, n), out_shape=jax.ShapeDtypeStr...]
    psum x1 -> x0, blocking collectives: 25.3 us -> none  [local_step(): attn_out = lax.psum(partial_out, 'sp').astype(jnp.bfloat16)]
    pmax x1 -> x0, blocking collectives: 24.1 us -> none  [local_step(): global_max = lax.pmax(local_max, 'sp')]
    unnamed x20 -> x4, local copies, waits for them, and re-layouts: 6.63 us -> 0.01 us
    select_n x1, other arithmetic: 7.33 us -> 2.88 us  [local_step(): v_next = jnp.where(at_pos, v_new[:, None], v_here)]
  transfers between devices with their start and end apart: 1 -> 0, of which waited for: 1 -> 0; matrix products, arithmetic and copies ran while one was open for 0% -> 0% of each run, Pallas kernels for 0% -> 0%
where the time goes in v2:
time: 32.4 us
  Pallas kernels  28.8 us (89%)
  other arithmetic  2.88 us (9%)
  between operations  0.7 us (2%)
    pallas_call x1, Pallas kernels, local_step(): pl.pallas_call(functools.partial(_attend, n), out_shape=jax.ShapeDtypeStr...  14.8 us
    pallas_call x1, Pallas kernels, local_step(): pl.pallas_call(functools.partial(_project, n), out_shape=(pltpu.VMEM((EAR...  13.3 us
    select_n x1, other arithmetic, local_step(): v_next = jnp.where(at_pos, v_new[:, None], v_here)  2.88 us

profile of v2, /device:TPU:97, one launch (start us, length us, event | category | flops | bytes accessed | tf_op | source)
XLA Modules:
  0.0 32.4 jit_solution(9731248311563434541)
XLA Ops:
  0.6 13.3 %project.1 = (f32[5,16,2048]{2,1,0:T(8,128)S(1)}, bf16[8,16,256]{2,1,0:T(8,128)(2,1)S(1)}, s32[8,256]{1,0:T(8,128)S(1)}, s32[8,256]{1,0:T(8,128)S(1)}, bf16[8,8,...) custom-call(bf16[8,3584]{1,0:T(8,128)(2,1)} %hid_ref.1, ...), custom_call_target="tpu_custom_call" | custom-call | flops 10000000000 | bytes 29360128 | tf_op jit(solution)/shard_map/project/pallas_call | solution.py:271
  14.0 2.9 %broadcast_select_fusion = (bf16[8,256,8,256]{3,2,1,0:T(8,128)(2,1)S(1)}, bf16[8,256,8,256]{3,2,1,0:T(8,128)(2,1)S(1)}) fusion(bf16[8,256,8,256]{3,2,1,0:T(8,128)(2,1)S(1)} %get-tuple-element.18, pred[8,256]{1,0:T(8,128)(4,1)S(1)} %broadcast_compare_fusion, bf16[8,8,256]{2,1,0:T(8,128)(2,1)S(1)} %get-tuple-element.17, ...), kind=kLoop, calls=%fused_computation | loop fusion | flops 8388608 | bytes 33622016 | tf_op jit(solution)/shard_map/jit(_where)/select_n | solution.py:301
  16.9 0.0 copy-start
  16.9 0.0 copy-start.1
  16.9 14.8 %attend.1.attn_ref = bf16[8,3584]{1,0:T(8,128)(2,1)S(1)} custom-call(f32[5,16,2048]{2,1,0:T(8,128)S(1)} %get-tuple-element.11.s_ref, bf16[8,16,256]{2,1,0:T(8,128)(2,1)S(1)} %get-tuple-element.12.q_ref, s32[8,256]{1,0:T(8,128)S(1)} %get-tuple-element.13.end_ref, bf16[8,256,8,256]{3,2,1,0:T(8,128)(2,1)S(1)} %get-tuple-element.20.k_ref, ...), custom_call_target="tpu_custom_call" | custom-call | flops 20000000000 | bytes 4194304 | tf_op jit(solution)/shard_map/attend/pallas_call | solution.py:304
  31.7 0.0 copy-done
  31.7 0.0 copy-done.1
  31.7 0.6 %hand_over.1 = bf16[8,3584]{1,0:T(8,128)(2,1)} custom-call(bf16[8,3584]{1,0:T(8,128)(2,1)S(1)} %attend.1.attn_ref, bf16[8,256,8,256]{3,2,1,0:T(8,128)(2,1)S(1)} %get-tuple-element.20.k_ref, bf16[8,256,8,256]{3,2,1,0:T(8,128)(2,1)S(1)} %get-tuple-element.19.v_ref), custom_call_target="tpu_custom_call" | custom-call | tf_op jit(solution)/shard_map/hand_over/pallas_call | solution.py:324
  (1 shorter events, 0.0 us)
Async XLA Ops:
  16.9 14.8 %copy-start = (bf16[8,256,8,256]{3,2,1,0:T(8,128)(2,1)}, bf16[8,256,8,256]{3,2,1,0:T(8,128)(2,1)S(1)}, u32[]{:S(2)}) copy-start(bf16[8,256,8,256]{3,2,1,0:T(8,128)(2,1)S(1)} %get-tuple-element.19.v_ref) | copy-start | bytes 25165828
  16.9 14.8 %copy-start.1 = (bf16[8,256,8,256]{3,2,1,0:T(8,128)(2,1)}, bf16[8,256,8,256]{3,2,1,0:T(8,128)(2,1)S(1)}, u32[]{:S(2)}) copy-start(bf16[8,256,8,256]{3,2,1,0:T(8,128)(2,1)S(1)} %get-tuple-element.20.k_ref) | copy-start | bytes 25165828

commit v3 on v2

v3 whole, which is shorter than its diff:
```python
import functools

import jax
import jax.numpy as jnp
from jax import lax
from jax.experimental import pallas as pl
from jax.experimental.pallas import tpu as pltpu
from jax.sharding import PartitionSpec as P

F32 = jnp.float32
BF16 = jnp.bfloat16
FLOOR = float(jnp.finfo(jnp.float32).min)
MESH = pl.DeviceIdType.MESH
Q_PARTS = (6, 5, 3)
KV_PARTS = (8, 6)
K_PARTS = 4
K_FIRST = 2
V_PARTS = 2
EARLY = 6
TILE = 32
LAG = 2
MIB = 1 << 20


def _peer(me, off, n):
    return lax.rem(me + off, n)


def _greet(me, n):
    barrier = pltpu.get_barrier_semaphore()
    for off in range(1, n):
        pl.semaphore_signal(barrier, inc=1, device_id={'sp': _peer(me, off, n)}, device_id_type=MESH)
    return barrier


def _far_first(n):
    return sorted(range(1, n), key=lambda off: abs(off - n // 2))


def _exchange(me, n, src, dst, ssem, rsem):
    def copy(off):
        peer = _peer(me, off, n)
        return pltpu.make_async_remote_copy(
            src_ref=src(peer), dst_ref=dst(off), send_sem=ssem.at[off - 1], recv_sem=rsem.at[off - 1],
            device_id={'sp': peer}, device_id_type=MESH)

    copies = [copy(off) for off in range(1, n)]
    for off in _far_first(n):
        copies[off - 1].start()
    return copies


def _part(i, size, parts):
    return pl.ds(i * size // parts, size // parts)


def _positions(heads, width, never):
    col = lax.broadcasted_iota(jnp.int32, (2 * heads, width), 1)
    row = lax.broadcasted_iota(jnp.int32, (2 * heads, width), 0)
    return jnp.where((col % heads) == (row % heads), col // heads, never)


def _rows(i, count):
    return pl.ds(pl.multiple_of(i * count, count), count)


def _project(n, hid_ref, wq_ref, wk_ref, wv_ref, kc_ref, vc_ref, wp_ref, vl_ref,
             s_ref, f_ref, q_ref, end_ref, at_ref, kn_ref, vn_ref, k_ref, v_ref,
             hid, wqb, wkb, wvb, acc, mine, got, full, wp, vl,
             hsem, qsem, wsem, ksem, vsem, psem, s1, r1, s2, r2):
    me = lax.axis_index('sp')
    rows, seq, heads, dim = k_ref.shape
    depth, qw = wqb.shape
    blocks = dim // 128
    w = TILE * heads
    small = [
        pltpu.make_async_copy(hid_ref, hid, hsem),
        pltpu.make_async_copy(wp_ref, wp, psem.at[0]),
        pltpu.make_async_copy(vl_ref, vl, psem.at[1]),
    ]

    def slices(parts):
        unit = depth // sum(parts)
        return [pl.ds(sum(parts[:c]) * unit, parts[c] * unit) for c in range(len(parts))]

    q_rows, kv_rows = slices(Q_PARTS), slices(KV_PARTS)
    q_copies = [pltpu.make_async_copy(wq_ref.at[r, _rows(me, qw)], wqb.at[r], qsem.at[c]) for c, r in enumerate(q_rows)]
    kv_copies = [
        pltpu.make_async_copy(src.at[r, _rows(me, dim)], dst.at[r], wsem.at[i, c])
        for c, r in enumerate(kv_rows) for i, (src, dst) in enumerate(((wk_ref, wkb), (wv_ref, wvb)))
    ]
    k_copies, v_copies = [
        [pltpu.make_async_copy(src.at[_part(i, rows, parts)], dst.at[_part(i, rows, parts)], sem.at[i]) for i in range(parts)]
        for src, dst, sem, parts in ((kc_ref, k_ref, ksem, K_PARTS), (vc_ref, v_ref, vsem, V_PARTS))
    ]
    for cp in q_copies + small:
        cp.start()
    barrier = _greet(me, n)

    def gathered(i, ssem, rsem):
        return _exchange(me, n, lambda peer: mine.at[i], lambda off: got.at[i, off - 1], ssem, rsem)

    def spread(i, src, value):
        value = value.astype(F32)
        for c in range(value.shape[1] // 128):
            full[i * 2 * blocks + c, _rows(src, rows), :] = value[:, c * 128:(c + 1) * 128]

    def collect(i, copies):
        for off in range(1, n):
            copies[off - 1].wait()
            spread(i, _peer(me, n - off, n), got[i, off - 1])

    for cp in small:
        cp.wait()
    for c, r in enumerate(q_rows):
        q_copies[c].wait()
        if c == 0:
            for cp in kv_copies:
                cp.start()
        if c == len(q_rows) - 1:
            for cp in k_copies[:K_FIRST]:
                cp.start()

        @pl.when(me >= 0)
        def _():
            part = jnp.dot(hid[:, r], wqb[r, :], preferred_element_type=F32)
            acc[:, :qw] = part if c == 0 else acc[:, :qw] + part

    mine[0] = acc[:, :qw].astype(BF16)
    pl.semaphore_wait(barrier, n - 1)
    x1 = gathered(0, s1, r1)
    for c, r in enumerate(kv_rows):
        for cp in kv_copies[2 * c:2 * c + 2]:
            cp.wait()
        if c == 0:
            for cp in k_copies[K_FIRST:]:
                cp.start()

        @pl.when(me >= 0)
        def _():
            part = jnp.concatenate([jnp.dot(hid[:, r], ref[r, :], preferred_element_type=F32) for ref in (wkb, wvb)], axis=1)
            acc[:, qw:] = part if c == 0 else acc[:, qw:] + part

    mine[1] = acc[:, qw:].astype(BF16)
    x2 = gathered(1, s2, r2)
    for cp in v_copies:
        cp.start()
    for i in range(2):
        spread(i, me, mine[i])
    collect(0, x1)

    def of_row(b, first):
        return jnp.concatenate([full[first * blocks + c, pl.ds(b, n, stride=rows), :] for c in range(blocks)], axis=1)

    def times(q, kt):
        return lax.dot_general(q, kt, (((1,), (1,)), ((), ())), preferred_element_type=F32) * scale

    colpos = _positions(heads, w, 2 * seq * n)
    scale = dim ** -0.5
    for cp in k_copies:
        cp.wait()
    for b in range(rows):
        q = jnp.concatenate([of_row(b, 0), of_row(b, 1)], axis=0).astype(BF16)
        q_ref[b] = q
        end = vl[b] - me * seq
        end_ref[b:b + 1, :] = jnp.full((1, w), end, jnp.int32)
        if b >= EARLY:
            continue
        for t in range(seq // TILE):
            s = times(q, k_ref[b, pl.ds(t * TILE, TILE)].reshape(w, dim))
            s_ref[b, :, t * w:(t + 1) * w] = jnp.where(colpos < end - t * TILE, s, -jnp.inf)
    collect(1, x2)
    for b in range(rows):
        kn = of_row(b, 2).astype(BF16)
        kn_ref[b] = kn
        vn_ref[b] = of_row(b, 3).astype(BF16)
        at_ref[b:b + 1, :] = jnp.full((1, w), wp[b] - me * seq, jnp.int32)
        if b >= EARLY:
            continue
        s = times(q_ref[b], jnp.concatenate([kn[None]] * TILE, axis=0).reshape(w, dim))
        f_ref[b] = jnp.where(wp[b] < vl[b], s, -jnp.inf)
    for cp in v_copies:
        cp.wait()


def _patch(at_ref, kn_ref, vn_ref, ki_ref, vi_ref, k_ref, v_ref):
    del ki_ref, vi_ref
    rows, seq = k_ref.shape[:2]
    for b in range(rows):
        at = at_ref[b, 0]

        @pl.when((at >= 0) & (at < seq))
        def _():
            k_ref[b, at] = kn_ref[b]
            v_ref[b, at] = vn_ref[b]


def _attend(n, s_ref, f_ref, q_ref, end_ref, at_ref, k_ref, v_ref, wo_ref, out_ref, w_ref, p_ref, xs, xr, part, recv, red, gath,
            wsem, s2, r2, s4, r4, s5, r5):
    me = lax.axis_index('sp')
    rows, seq, heads, dim = v_ref.shape
    model = out_ref.shape[1]
    cols = red.shape[1]
    blocks = dim // 128
    ntile = seq // TILE
    w = TILE * heads
    span = xs.shape[0] // heads
    wcopy = pltpu.make_async_copy(wo_ref, w_ref.at[:, pl.ds(0, model)], wsem)
    wcopy.start()
    w_ref[:, model:] = jnp.zeros((w_ref.shape[0], n * cols - model), BF16)
    barrier = _greet(me, n)
    lane = lax.broadcasted_iota(jnp.int32, (heads, 128), 1)
    colpos = _positions(heads, w, 2 * seq * n)
    scale = dim ** -0.5

    def soften(b):
        if b < EARLY:
            at = at_ref[b:b + 1, :]
            fresh = f_ref[b]
            ss = [jnp.where(colpos == at - t * TILE, fresh, s_ref[b, :, t * w:(t + 1) * w]) for t in range(ntile)]
        else:
            end = end_ref[b:b + 1, :]
            ss = [lax.dot_general(q_ref[b], k_ref[b, pl.ds(t * TILE, TILE)].reshape(w, dim), (((1,), (1,)), ((), ())),
                                  preferred_element_type=F32) * scale for t in range(ntile)]
            ss = [jnp.where(colpos < end - t * TILE, s, -jnp.inf) for t, s in enumerate(ss)]
        m = jnp.max(functools.reduce(jnp.maximum, ss), axis=-1, keepdims=True)
        m = jnp.maximum(m, FLOOR)
        ps = [jnp.exp(s - m) for s in ss]
        l = jnp.sum(functools.reduce(jnp.add, ps), axis=-1, keepdims=True)
        for t in range(ntile):
            p_ref[b, :, t * w:(t + 1) * w] = ps[t].astype(BF16)
        st = jnp.where(lane == 0, m[:heads], jnp.where(lane == 1, l[:heads], jnp.where(lane == 2, m[heads:], l[heads:])))
        xs[pl.ds(blocks * 2 * rows + b, heads, stride=span), :] = st

    def values(b):
        acc = functools.reduce(jnp.add, [
            functools.reduce(jnp.add, [
                jnp.dot(p_ref[b, :, t * w:(t + 1) * w], v_ref[b, pl.ds(t * TILE, TILE)].reshape(w, dim),
                        preferred_element_type=F32) for t in range(first, ntile, 2)]) for first in range(2)])
        for c in range(blocks):
            piece = acc[:, c * 128:(c + 1) * 128]
            xs[pl.ds(c * 2 * rows + b, heads, stride=span), :] = piece[:heads]
            xs[pl.ds(c * 2 * rows + rows + b, heads, stride=span), :] = piece[heads:]

    for i in range(rows + LAG):
        if i < rows:
            soften(i)
        if i >= LAG:
            values(i - LAG)
    pl.semaphore_wait(barrier, n - 1)
    x2 = _exchange(me, n, lambda peer: xs.at[_rows(peer, span)], lambda off: xr.at[off - 1], s2, r2)
    xr[n - 1] = xs[_rows(me, span), :]
    for cp in x2:
        cp.wait()
    base = blocks * 2 * rows
    pieces = []
    sts = [xr[i, base:base + rows, :] for i in range(n)]
    for j in range(2):
        ms = [st[:, 2 * j:2 * j + 1] for st in sts]
        top = functools.reduce(jnp.maximum, ms)
        es = [jnp.exp(m - top) for m in ms]
        total = functools.reduce(jnp.add, [st[:, 2 * j + 1:2 * j + 2] * e for st, e in zip(sts, es)])
        for c in range(blocks):
            at = c * 2 * rows + j * rows
            num = functools.reduce(jnp.add, [xr[i, at:at + rows, :] * es[i] for i in range(n)])
            pieces.append((num / total).astype(BF16))
    o = jnp.concatenate(pieces, axis=1)
    wcopy.wait()

    def block(i):
        return jnp.dot(o, w_ref[:, _rows(i, cols)], preferred_element_type=F32)

    rs = []
    for off in _far_first(n):
        peer = _peer(me, off, n)
        part[off - 1] = block(peer)
        rs.append(pltpu.make_async_remote_copy(
            src_ref=part.at[off - 1], dst_ref=recv.at[off - 1], send_sem=s4.at[off - 1], recv_sem=r4.at[off - 1],
            device_id={'sp': peer}, device_id_type=MESH))
        rs[-1].start()
    total = block(me)
    for off in range(1, n):
        rs[_far_first(n).index(off)].wait()
        total += recv[off - 1]
    red[...] = total.astype(BF16)
    ag = _exchange(me, n, lambda peer: red, lambda off: gath.at[:, _rows(me, cols)], s5, r5)
    for cp in ag:
        cp.wait()
    gath[:, _rows(me, cols)] = red[...]
    out_ref[...] = gath[:, :model]


def _hand_over(attn_ref, k_ref, v_ref, out_ref):
    del k_ref, v_ref
    out_ref[...] = attn_ref[...]


def solution(mesh):
    row_spec = P(('rep', 'dp'), None)
    cache_spec = P(('rep', 'dp'), 'sp', None, None)
    len_spec = P(('rep', 'dp'))
    n = mesh.shape['sp']
    vmem = pl.BlockSpec(memory_space=pltpu.VMEM)
    hbm = pl.BlockSpec(memory_space=pltpu.HBM)
    dma = pltpu.SemaphoreType.DMA

    def in_hbm(x):
        return pltpu.with_memory_space_constraint(x, pltpu.HBM)

    def local_step(hidden, w_query, w_key, w_value, w_out, k_cache, v_cache, write_pos, valid_len):
        rows, seq, heads, dim = k_cache.shape
        depth = hidden.shape[1]
        model = w_out.shape[1]
        qw = w_query.shape[1] // n
        lw = qw + 2 * dim
        blocks = dim // 128
        cache = pltpu.VMEM(k_cache.shape, BF16)
        new = pltpu.VMEM((rows, heads, dim), BF16)
        scores, fresh, query, ends, at, k_new, v_new, k_here, v_here = pl.pallas_call(
            functools.partial(_project, n),
            out_shape=(
                pltpu.VMEM((EARLY, 2 * heads, seq * heads), F32),
                pltpu.VMEM((EARLY, 2 * heads, TILE * heads), F32),
                pltpu.VMEM((rows, 2 * heads, dim), BF16),
                pltpu.VMEM((rows, TILE * heads), jnp.int32),
                pltpu.VMEM((rows, TILE * heads), jnp.int32),
                new, new, cache, cache,
            ),
            in_specs=[hbm] * 8,
            out_specs=(vmem,) * 9,
            scratch_shapes=[
                pltpu.VMEM((rows, depth), BF16),
                pltpu.VMEM((depth, qw), BF16),
                pltpu.VMEM((depth, dim), BF16),
                pltpu.VMEM((depth, dim), BF16),
                pltpu.VMEM((rows, lw), F32),
                pltpu.VMEM((2, rows, lw // 2), BF16),
                pltpu.VMEM((2, n - 1, rows, lw // 2), BF16),
                pltpu.VMEM((lw // 128, n * rows, 128), F32),
                pltpu.SMEM((rows,), jnp.int32),
                pltpu.SMEM((rows,), jnp.int32),
                dma, dma((len(Q_PARTS),)), dma((2, len(KV_PARTS))), dma((K_PARTS,)), dma((V_PARTS,)), dma((2,)),
            ] + [dma((n - 1,))] * 4,
            compiler_params=pltpu.CompilerParams(collective_id=0, has_side_effects=True, vmem_limit_bytes=12 * MIB),
            cost_estimate=pl.CostEstimate(flops=10_000_000_000, bytes_accessed=28 * MIB, transcendentals=0),
            name='project',
        )(*[in_hbm(x) for x in (hidden, w_query, w_key, w_value, k_cache, v_cache, write_pos, valid_len)])
        k_here, v_here = pl.pallas_call(
            _patch,
            out_shape=(cache, cache),
            in_specs=[vmem] * 5,
            out_specs=(vmem, vmem),
            input_output_aliases={3: 0, 4: 1},
            compiler_params=pltpu.CompilerParams(vmem_limit_bytes=1 * MIB),
            name='patch',
        )(at, k_new, v_new, k_here, v_here)
        top = lax.optimization_barrier(jnp.full((), jnp.inf, BF16))
        k_next = jnp.minimum(k_here, top)
        v_next = jnp.minimum(v_here, top)
        padded = -(-model // (128 * n)) * 128 * n
        span = 2 * rows * blocks + rows
        attn = pl.pallas_call(
            functools.partial(_attend, n),
            out_shape=jax.ShapeDtypeStruct((rows, model), BF16),
            in_specs=[vmem] * 7 + [hbm],
            out_specs=vmem,
            scratch_shapes=[
                pltpu.VMEM((w_out.shape[0], padded), BF16),
                pltpu.VMEM((rows, 2 * heads, seq * heads), BF16),
                pltpu.VMEM((heads * span, 128), F32),
                pltpu.VMEM((n, span, 128), F32),
                pltpu.VMEM((n - 1, rows, padded // n), F32),
                pltpu.VMEM((n - 1, rows, padded // n), F32),
                pltpu.VMEM((rows, padded // n), BF16),
                pltpu.VMEM((rows, padded), BF16),
                dma,
            ] + [dma((n - 1,))] * 6,
            compiler_params=pltpu.CompilerParams(collective_id=1, has_side_effects=True, vmem_limit_bytes=8 * MIB),
            cost_estimate=pl.CostEstimate(flops=20_000_000_000, bytes_accessed=4 * MIB, transcendentals=0),
            name='attend',
        )(scores, fresh, query, ends, at, k_next, v_next, in_hbm(w_out))
        attn = pl.pallas_call(
            _hand_over,
            out_shape=jax.ShapeDtypeStruct((rows, model), BF16),
            in_specs=[vmem] * 3,
            out_specs=vmem,
            compiler_params=pltpu.CompilerParams(vmem_limit_bytes=1 * MIB),
            name='hand_over',
        )(attn, k_next, v_next)
        return attn, k_next, v_next

    return jax.shard_map(
        local_step, mesh=mesh,
        in_specs=(row_spec, P(), P(), P(), P('sp', None), cache_spec, cache_spec, len_spec, len_spec),
        out_specs=(row_spec, cache_spec, cache_spec), check_vma=False)
```

time: 32.4 us -> 29.3 us (0.904)
  other arithmetic: 2.88 us -> 1.16 us
  Pallas kernels: 28.8 us -> 27.3 us
    select_n x1 -> x0, other arithmetic: 2.88 us -> none  [local_step(): v_next = jnp.where(at_pos, v_new[:, None], v_here)]
    pallas_call x1, Pallas kernels: 13.3 us -> 11.3 us  [local_step(): pl.pallas_call(functools.partial(_project, n), out_shape=(pltpu.VMEM((EAR...]
    min x0 -> x1, other arithmetic: none -> 1.16 us  [local_step(): v_next = jnp.minimum(v_here, top)]
where the time goes in v3:
time: 29.3 us; the launch traced here: 29.2 us
  Pallas kernels  27.3 us (93%)
  other arithmetic  1.16 us (4%)
  between operations  0.7 us (2%)
    pallas_call x1, Pallas kernels, local_step(): pl.pallas_call(functools.partial(_attend, n), out_shape=jax.ShapeDtypeStr...  15.1 us
    pallas_call x1, Pallas kernels, local_step(): pl.pallas_call(functools.partial(_project, n), out_shape=(pltpu.VMEM((EAR...  11.3 us
    min x1, other arithmetic, local_step(): v_next = jnp.minimum(v_here, top)  1.16 us
    pallas_call x1, Pallas kernels, local_step(): pl.pallas_call(_hand_over, out_shape=jax.ShapeDtypeStruct((rows, model),...  0.63 us

profile of v3, /device:TPU:97, one launch (start us, length us, event | category | flops | bytes accessed | tf_op | source)
XLA Modules:
  0.0 29.2 jit_solution(13276001438577187825)
XLA Ops:
  0.6 11.3 %project.1 = (f32[6,16,2048]{2,1,0:T(8,128)S(1)}, f32[6,16,256]{2,1,0:T(8,128)S(1)}, bf16[8,16,256]{2,1,0:T(8,128)(2,1)S(1)}, s32[8,256]{1,0:T(8,128)S(1)}, s32[...) custom-call(bf16[8,3584]{1,0:T(8,128)(2,1)} %hid_ref.1, ...), custom_call_target="tpu_custom_call" | custom-call | flops 10000000000 | bytes 29360128 | tf_op jit(solution)/shard_map/project/pallas_call | solution.py:319
  12.0 0.3 %patch.1 = (bf16[8,256,8,256]{3,2,1,0:T(8,128)(2,1)S(1)}, bf16[8,256,8,256]{3,2,1,0:T(8,128)(2,1)S(1)}) custom-call(s32[8,256]{1,0:T(8,128)S(1)} %get-tuple-element.18.at_ref, bf16[8,8,256]{2,1,0:T(8,128)(2,1)S(1)} %get-tuple-element.19.kn_ref, bf16[8,8,256]{2,1,0:T(8,128)(2,1)S(1)} %get-tuple-element.20.vn_ref, ...), custom_call_target="tpu_custom_call", output_to_operand_aliasing={{0}: (3, {}), {1}: (4, {})} | custom-call | tf_op jit(solution)/shard_map/patch/pallas_call | solution.py:348
  12.3 1.2 %broadcast_minimum_fusion = (bf16[8,256,8,256]{3,2,1,0:T(8,128)(2,1)S(1)}, bf16[8,256,8,256]{3,2,1,0:T(8,128)(2,1)S(1)}) fusion(bf16[8,256,8,256]{3,2,1,0:T(8,128)(2,1)S(1)} %get-tuple-element.24, bf16[]{:T(256)} %constant.0.clone.1, bf16[8,256,8,256]{3,2,1,0:T(8,128)(2,1)S(1)} %get-tuple-element.23), kind=kLoop, calls=%fused_computation | loop fusion | flops 8388608 | bytes 33554432 | tf_op jit(solution)/shard_map/min | solution.py:359
  13.5 0.0 copy-start
  13.5 0.0 copy-start.1
  13.5 15.1 %attend.1.attn_ref = bf16[8,3584]{1,0:T(8,128)(2,1)S(1)} custom-call(f32[6,16,2048]{2,1,0:T(8,128)S(1)} %get-tuple-element.14.s_ref, f32[6,16,256]{2,1,0:T(8,128)S(1)} %get-tuple-element.15.f_ref, bf16[8,16,256]{2,1,0:T(8,128)(2,1)S(1)} %get-tuple-element.16.q_ref, s32[8,256]{1,0:T(8,128)S(1)} %get-tuple-element.17.end_ref, ...), custom_call_target="tpu_custom_call" | custom-call | flops 20000000000 | bytes 4194304 | tf_op jit(solution)/shard_map/attend/pallas_call | solution.py:362
  28.6 0.0 copy-done
  28.6 0.0 copy-done.1
  28.6 0.6 %hand_over.1 = bf16[8,3584]{1,0:T(8,128)(2,1)} custom-call(bf16[8,3584]{1,0:T(8,128)(2,1)S(1)} %attend.1.attn_ref, bf16[8,256,8,256]{3,2,1,0:T(8,128)(2,1)S(1)} %get-tuple-element.26.k_ref, bf16[8,256,8,256]{3,2,1,0:T(8,128)(2,1)S(1)} %get-tuple-element.25.v_ref), custom_call_target="tpu_custom_call" | custom-call | tf_op jit(solution)/shard_map/hand_over/pallas_call | solution.py:382
Async XLA Ops:
  13.5 15.1 %copy-start = (bf16[8,256,8,256]{3,2,1,0:T(8,128)(2,1)}, bf16[8,256,8,256]{3,2,1,0:T(8,128)(2,1)S(1)}, u32[]{:S(2)}) copy-start(bf16[8,256,8,256]{3,2,1,0:T(8,128)(2,1)S(1)} %get-tuple-element.25.v_ref) | copy-start | bytes 25165828
  13.5 15.1 %copy-start.1 = (bf16[8,256,8,256]{3,2,1,0:T(8,128)(2,1)}, bf16[8,256,8,256]{3,2,1,0:T(8,128)(2,1)S(1)}, u32[]{:S(2)}) copy-start(bf16[8,256,8,256]{3,2,1,0:T(8,128)(2,1)S(1)} %get-tuple-element.26.k_ref) | copy-start | bytes 25165828

commit v4 on v3

--- a/solution.py
+++ b/solution.py
@@ -16,7 +16,8 @@
 K_PARTS = 4
 K_FIRST = 2
 V_PARTS = 2
-EARLY = 6
+EARLY = 7
+FAR = 2
 TILE = 32
 LAG = 2
 MIB = 1 << 20
@@ -37,17 +38,21 @@
     return sorted(range(1, n), key=lambda off: abs(off - n // 2))
 
 
-def _exchange(me, n, src, dst, ssem, rsem):
-    def copy(off):
-        peer = _peer(me, off, n)
-        return pltpu.make_async_remote_copy(
-            src_ref=src(peer), dst_ref=dst(off), send_sem=ssem.at[off - 1], recv_sem=rsem.at[off - 1],
-            device_id={'sp': peer}, device_id_type=MESH)
-
-    copies = [copy(off) for off in range(1, n)]
+def _send(me, n, off, src, dst, sems):
+    peer = _peer(me, off, n)
+    pltpu.make_async_remote_copy(
+        src_ref=src(peer), dst_ref=dst(off), send_sem=sems.at[0], recv_sem=sems.at[1],
+        device_id={'sp': peer}, device_id_type=MESH).start()
+
+
+def _exchange(me, n, src, dst, sems):
     for off in _far_first(n):
-        copies[off - 1].start()
-    return copies
+        _send(me, n, off, src, dst, sems)
+
+
+def _settle(total, sems):
+    for i in range(2):
+        pltpu.make_async_copy(total, total, sems.at[i]).wait()
 
 
 def _part(i, size, parts):
@@ -67,7 +72,7 @@
 def _project(n, hid_ref, wq_ref, wk_ref, wv_ref, kc_ref, vc_ref, wp_ref, vl_ref,
              s_ref, f_ref, q_ref, end_ref, at_ref, kn_ref, vn_ref, k_ref, v_ref,
              hid, wqb, wkb, wvb, acc, mine, got, full, wp, vl,
-             hsem, qsem, wsem, ksem, vsem, psem, s1, r1, s2, r2):
+             hsem, qsem, wsem, ksem, vsem, psem, x1, x2):
     me = lax.axis_index('sp')
     rows, seq, heads, dim = k_ref.shape
     depth, qw = wqb.shape
@@ -97,17 +102,17 @@
         cp.start()
     barrier = _greet(me, n)
 
-    def gathered(i, ssem, rsem):
-        return _exchange(me, n, lambda peer: mine.at[i], lambda off: got.at[i, off - 1], ssem, rsem)
+    def gather(i, sems):
+        _exchange(me, n, lambda peer: mine.at[i], lambda off: got.at[i, off - 1], sems)
 
     def spread(i, src, value):
         value = value.astype(F32)
         for c in range(value.shape[1] // 128):
             full[i * 2 * blocks + c, _rows(src, rows), :] = value[:, c * 128:(c + 1) * 128]
 
-    def collect(i, copies):
+    def collect(i, sems):
+        _settle(got.at[i], sems)
         for off in range(1, n):
-            copies[off - 1].wait()
             spread(i, _peer(me, n - off, n), got[i, off - 1])
 
     for cp in small:
@@ -128,7 +133,7 @@
 
     mine[0] = acc[:, :qw].astype(BF16)
     pl.semaphore_wait(barrier, n - 1)
-    x1 = gathered(0, s1, r1)
+    gather(0, x1)
     for c, r in enumerate(kv_rows):
         for cp in kv_copies[2 * c:2 * c + 2]:
             cp.wait()
@@ -142,7 +147,7 @@
             acc[:, qw:] = part if c == 0 else acc[:, qw:] + part
 
     mine[1] = acc[:, qw:].astype(BF16)
-    x2 = gathered(1, s2, r2)
+    gather(1, x2)
     for cp in v_copies:
         cp.start()
     for i in range(2):
@@ -196,7 +201,7 @@
 
 
 def _attend(n, s_ref, f_ref, q_ref, end_ref, at_ref, k_ref, v_ref, wo_ref, out_ref, w_ref, p_ref, xs, xr, part, recv, red, gath,
-            wsem, s2, r2, s4, r4, s5, r5):
+            wsem, x2, x3, x4):
     me = lax.axis_index('sp')
     rows, seq, heads, dim = v_ref.shape
     model = out_ref.shape[1]
@@ -248,10 +253,9 @@
         if i >= LAG:
             values(i - LAG)
     pl.semaphore_wait(barrier, n - 1)
-    x2 = _exchange(me, n, lambda peer: xs.at[_rows(peer, span)], lambda off: xr.at[off - 1], s2, r2)
+    _exchange(me, n, lambda peer: xs.at[_rows(peer, span)], lambda off: xr.at[off - 1], x2)
     xr[n - 1] = xs[_rows(me, span), :]
-    for cp in x2:
-        cp.wait()
+    _settle(xr.at[pl.ds(0, n - 1)], x2)
     base = blocks * 2 * rows
     pieces = []
     sts = [xr[i, base:base + rows, :] for i in range(n)]
@@ -267,25 +271,19 @@
     o = jnp.concatenate(pieces, axis=1)
     wcopy.wait()
 
-    def block(i):
-        return jnp.dot(o, w_ref[:, _rows(i, cols)], preferred_element_type=F32)
-
-    rs = []
-    for off in _far_first(n):
-        peer = _peer(me, off, n)
-        part[off - 1] = block(peer)
-        rs.append(pltpu.make_async_remote_copy(
-            src_ref=part.at[off - 1], dst_ref=recv.at[off - 1], send_sem=s4.at[off - 1], recv_sem=r4.at[off - 1],
-            device_id={'sp': peer}, device_id_type=MESH))
-        rs[-1].start()
-    total = block(me)
+    order = _far_first(n)
+    for group in (order[:FAR], order[FAR:]):
+        for off in group:
+            part[off - 1] = jnp.dot(o, w_ref[:, _rows(_peer(me, off, n), cols)], preferred_element_type=F32)
+        for off in group:
+            _send(me, n, off, lambda peer: part.at[off - 1], lambda off: recv.at[off - 1], x3)
+    total = jnp.dot(o, w_ref[:, _rows(me, cols)], preferred_element_type=F32)
+    _settle(recv, x3)
     for off in range(1, n):
-        rs[_far_first(n).index(off)].wait()
         total += recv[off - 1]
     red[...] = total.astype(BF16)
-    ag = _exchange(me, n, lambda peer: red, lambda off: gath.at[:, _rows(me, cols)], s5, r5)
-    for cp in ag:
-        cp.wait()
+    _exchange(me, n, lambda peer: red, lambda off: gath.at[:, _rows(me, cols)], x4)
+    _settle(gath.at[:, pl.ds(0, (n - 1) * cols)], x4)
     gath[:, _rows(me, cols)] = red[...]
     out_ref[...] = gath[:, :model]
 
@@ -340,7 +338,8 @@
                 pltpu.SMEM((rows,), jnp.int32),
                 pltpu.SMEM((rows,), jnp.int32),
                 dma, dma((len(Q_PARTS),)), dma((2, len(KV_PARTS))), dma((K_PARTS,)), dma((V_PARTS,)), dma((2,)),
-            ] + [dma((n - 1,))] * 4,
+                dma((2,)), dma((2,)),
+            ],
             compiler_params=pltpu.CompilerParams(collective_id=0, has_side_effects=True, vmem_limit_bytes=12 * MIB),
             cost_estimate=pl.CostEstimate(flops=10_000_000_000, bytes_accessed=28 * MIB, transcendentals=0),
             name='project',
@@ -373,8 +372,8 @@
                 pltpu.VMEM((n - 1, rows, padded // n), F32),
                 pltpu.VMEM((rows, padded // n), BF16),
                 pltpu.VMEM((rows, padded), BF16),
-                dma,
-            ] + [dma((n - 1,))] * 6,
+                dma, dma((2,)), dma((2,)), dma((2,)),
+            ],
             compiler_params=pltpu.CompilerParams(collective_id=1, has_side_effects=True, vmem_limit_bytes=8 * MIB),
             cost_estimate=pl.CostEstimate(flops=20_000_000_000, bytes_accessed=4 * MIB, transcendentals=0),
             name='attend',

time: 29.3 us -> 28.7 us (0.980)
  Pallas kernels: 27.3 us -> 26.8 us
    pallas_call x1, Pallas kernels: 15.1 us -> 14.4 us  [local_step(): pl.pallas_call(functools.partial(_attend, n), out_shape=jax.ShapeDtypeStr...]
where the time goes in v4:
time: 28.7 us; the launch traced here: 28.6 us
  Pallas kernels  26.8 us (93%)
  other arithmetic  1.16 us (4%)
  between operations  0.7 us (2%)
    pallas_call x1, Pallas kernels, local_step(): pl.pallas_call(functools.partial(_attend, n), out_shape=jax.ShapeDtypeStr...  14.4 us
    pallas_call x1, Pallas kernels, local_step(): pl.pallas_call(functools.partial(_project, n), out_shape=(pltpu.VMEM((EAR...  11.4 us
    min x1, other arithmetic, local_step(): v_next = jnp.minimum(v_here, top)  1.16 us
    pallas_call x1, Pallas kernels, local_step(): pl.pallas_call(_hand_over, out_shape=jax.ShapeDtypeStruct((rows, model),...  0.63 us

profile of v4, /device:TPU:97, one launch (start us, length us, event | category | flops | bytes accessed | tf_op | source)
XLA Modules:
  0.0 28.6 jit_solution(13229027829601293605)
XLA Ops:
  0.6 11.4 %project.1 = (f32[7,16,2048]{2,1,0:T(8,128)S(1)}, f32[7,16,256]{2,1,0:T(8,128)S(1)}, bf16[8,16,256]{2,1,0:T(8,128)(2,1)S(1)}, s32[8,256]{1,0:T(8,128)S(1)}, s32[...) custom-call(bf16[8,3584]{1,0:T(8,128)(2,1)} %hid_ref.1, ...), custom_call_target="tpu_custom_call" | custom-call | flops 10000000000 | bytes 29360128 | tf_op jit(solution)/shard_map/project/pallas_call | solution.py:317
  12.1 0.3 %patch.1 = (bf16[8,256,8,256]{3,2,1,0:T(8,128)(2,1)S(1)}, bf16[8,256,8,256]{3,2,1,0:T(8,128)(2,1)S(1)}) custom-call(s32[8,256]{1,0:T(8,128)S(1)} %get-tuple-element.18.at_ref, bf16[8,8,256]{2,1,0:T(8,128)(2,1)S(1)} %get-tuple-element.19.kn_ref, bf16[8,8,256]{2,1,0:T(8,128)(2,1)S(1)} %get-tuple-element.20.vn_ref, ...), custom_call_target="tpu_custom_call", output_to_operand_aliasing={{0}: (3, {}), {1}: (4, {})} | custom-call | tf_op jit(solution)/shard_map/patch/pallas_call | solution.py:347
  12.4 1.2 %broadcast_minimum_fusion = (bf16[8,256,8,256]{3,2,1,0:T(8,128)(2,1)S(1)}, bf16[8,256,8,256]{3,2,1,0:T(8,128)(2,1)S(1)}) fusion(bf16[8,256,8,256]{3,2,1,0:T(8,128)(2,1)S(1)} %get-tuple-element.24, bf16[]{:T(256)} %constant.0.clone.1, bf16[8,256,8,256]{3,2,1,0:T(8,128)(2,1)S(1)} %get-tuple-element.23), kind=kLoop, calls=%fused_computation | loop fusion | flops 8388608 | bytes 33554432 | tf_op jit(solution)/shard_map/min | solution.py:358
  13.6 0.0 copy-start
  13.6 0.0 copy-start.1
  13.6 14.4 %attend.1.attn_ref = bf16[8,3584]{1,0:T(8,128)(2,1)S(1)} custom-call(f32[7,16,2048]{2,1,0:T(8,128)S(1)} %get-tuple-element.14.s_ref, f32[7,16,256]{2,1,0:T(8,128)S(1)} %get-tuple-element.15.f_ref, bf16[8,16,256]{2,1,0:T(8,128)(2,1)S(1)} %get-tuple-element.16.q_ref, s32[8,256]{1,0:T(8,128)S(1)} %get-tuple-element.17.end_ref, ...), custom_call_target="tpu_custom_call" | custom-call | flops 20000000000 | bytes 4194304 | tf_op jit(solution)/shard_map/attend/pallas_call | solution.py:361
  28.0 0.0 copy-done
  28.0 0.0 copy-done.1
  28.0 0.6 %hand_over.1 = bf16[8,3584]{1,0:T(8,128)(2,1)} custom-call(bf16[8,3584]{1,0:T(8,128)(2,1)S(1)} %attend.1.attn_ref, bf16[8,256,8,256]{3,2,1,0:T(8,128)(2,1)S(1)} %get-tuple-element.26.k_ref, bf16[8,256,8,256]{3,2,1,0:T(8,128)(2,1)S(1)} %get-tuple-element.25.v_ref), custom_call_target="tpu_custom_call" | custom-call | tf_op jit(solution)/shard_map/hand_over/pallas_call | solution.py:381
Async XLA Ops:
  13.6 14.4 %copy-start = (bf16[8,256,8,256]{3,2,1,0:T(8,128)(2,1)}, bf16[8,256,8,256]{3,2,1,0:T(8,128)(2,1)S(1)}, u32[]{:S(2)}) copy-start(bf16[8,256,8,256]{3,2,1,0:T(8,128)(2,1)S(1)} %get-tuple-element.25.v_ref) | copy-start | bytes 25165828
  13.6 14.4 %copy-start.1 = (bf16[8,256,8,256]{3,2,1,0:T(8,128)(2,1)}, bf16[8,256,8,256]{3,2,1,0:T(8,128)(2,1)S(1)}, u32[]{:S(2)}) copy-start(bf16[8,256,8,256]{3,2,1,0:T(8,128)(2,1)S(1)} %get-tuple-element.26.k_ref) | copy-start | bytes 25165828

commit v5 on v4

--- a/solution.py
+++ b/solution.py
@@ -13,13 +13,13 @@
 MESH = pl.DeviceIdType.MESH
 Q_PARTS = (6, 5, 3)
 KV_PARTS = (8, 6)
-K_PARTS = 4
-K_FIRST = 2
-V_PARTS = 2
+K_PARTS = 2
+K_FIRST = 1
+V_PARTS = 1
 EARLY = 7
-FAR = 2
+GROUPS = ((0,), (1, 2), (3, 4), (5, 6))
 TILE = 32
-LAG = 2
+LAG = 3
 MIB = 1 << 20
 
 
@@ -191,9 +191,8 @@
 def _patch(at_ref, kn_ref, vn_ref, ki_ref, vi_ref, k_ref, v_ref):
     del ki_ref, vi_ref
     rows, seq = k_ref.shape[:2]
-    for b in range(rows):
-        at = at_ref[b, 0]
-
+    ats = [at_ref[b, 0] for b in range(rows)]
+    for b, at in enumerate(ats):
         @pl.when((at >= 0) & (at < seq))
         def _():
             k_ref[b, at] = kn_ref[b]
@@ -272,13 +271,16 @@
     wcopy.wait()
 
     order = _far_first(n)
-    for group in (order[:FAR], order[FAR:]):
-        for off in group:
+    for group in GROUPS:
+        for i in group:
+            off = order[i]
             part[off - 1] = jnp.dot(o, w_ref[:, _rows(_peer(me, off, n), cols)], preferred_element_type=F32)
-        for off in group:
+        for i in group:
+            off = order[i]
             _send(me, n, off, lambda peer: part.at[off - 1], lambda off: recv.at[off - 1], x3)
-    total = jnp.dot(o, w_ref[:, _rows(me, cols)], preferred_element_type=F32)
+    part[n - 1] = jnp.dot(o, w_ref[:, _rows(me, cols)], preferred_element_type=F32)
     _settle(recv, x3)
+    total = part[n - 1]
     for off in range(1, n):
         total += recv[off - 1]
     red[...] = total.astype(BF16)
@@ -368,7 +370,7 @@
                 pltpu.VMEM((rows, 2 * heads, seq * heads), BF16),
                 pltpu.VMEM((heads * span, 128), F32),
                 pltpu.VMEM((n, span, 128), F32),
-                pltpu.VMEM((n - 1, rows, padded // n), F32),
+                pltpu.VMEM((n, rows, padded // n), F32),
                 pltpu.VMEM((n - 1, rows, padded // n), F32),
                 pltpu.VMEM((rows, padded // n), BF16),
                 pltpu.VMEM((rows, padded), BF16),

time: 28.7 us -> 28 us (0.976)
  Pallas kernels: 26.8 us -> 26.1 us
    pallas_call x1, Pallas kernels: 14.4 us -> 13.9 us  [local_step(): pl.pallas_call(functools.partial(_attend, n), out_shape=jax.ShapeDtypeStr...]
where the time goes in v5:
time: 28 us; the launch traced here: 27.9 us
  Pallas kernels  26.1 us (93%)
  other arithmetic  1.16 us (4%)
  between operations  0.7 us (2%)
    pallas_call x1, Pallas kernels, local_step(): pl.pallas_call(functools.partial(_attend, n), out_shape=jax.ShapeDtypeStr...  13.9 us
    pallas_call x1, Pallas kernels, local_step(): pl.pallas_call(functools.partial(_project, n), out_shape=(pltpu.VMEM((EAR...  11.4 us
    min x1, other arithmetic, local_step(): v_next = jnp.minimum(v_here, top)  1.16 us
    pallas_call x1, Pallas kernels, local_step(): pl.pallas_call(_hand_over, out_shape=jax.ShapeDtypeStruct((rows, model),...  0.63 us

profile of v5, /device:TPU:97, one launch (start us, length us, event | category | flops | bytes accessed | tf_op | source)
XLA Modules:
  0.0 27.9 jit_solution(14527974457116217390)
XLA Ops:
  0.6 11.4 %project.1 = (f32[7,16,2048]{2,1,0:T(8,128)S(1)}, f32[7,16,256]{2,1,0:T(8,128)S(1)}, bf16[8,16,256]{2,1,0:T(8,128)(2,1)S(1)}, s32[8,256]{1,0:T(8,128)S(1)}, s32[...) custom-call(bf16[8,3584]{1,0:T(8,128)(2,1)} %hid_ref.1, ...), custom_call_target="tpu_custom_call" | custom-call | flops 10000000000 | bytes 29360128 | tf_op jit(solution)/shard_map/project/pallas_call | solution.py:319
  12.0 0.1 patch.1
  12.1 1.2 %broadcast_minimum_fusion = (bf16[8,256,8,256]{3,2,1,0:T(8,128)(2,1)S(1)}, bf16[8,256,8,256]{3,2,1,0:T(8,128)(2,1)S(1)}) fusion(bf16[8,256,8,256]{3,2,1,0:T(8,128)(2,1)S(1)} %get-tuple-element.24, bf16[]{:T(256)} %constant.0.clone.1, bf16[8,256,8,256]{3,2,1,0:T(8,128)(2,1)S(1)} %get-tuple-element.23), kind=kLoop, calls=%fused_computation | loop fusion | flops 8388608 | bytes 33554432 | tf_op jit(solution)/shard_map/min | solution.py:360
  13.3 0.0 copy-start
  13.3 0.0 copy-start.1
  13.3 13.9 %attend.1.attn_ref = bf16[8,3584]{1,0:T(8,128)(2,1)S(1)} custom-call(f32[7,16,2048]{2,1,0:T(8,128)S(1)} %get-tuple-element.14.s_ref, f32[7,16,256]{2,1,0:T(8,128)S(1)} %get-tuple-element.15.f_ref, bf16[8,16,256]{2,1,0:T(8,128)(2,1)S(1)} %get-tuple-element.16.q_ref, s32[8,256]{1,0:T(8,128)S(1)} %get-tuple-element.17.end_ref, ...), custom_call_target="tpu_custom_call" | custom-call | flops 20000000000 | bytes 4194304 | tf_op jit(solution)/shard_map/attend/pallas_call | solution.py:363
  27.3 0.0 copy-done
  27.3 0.0 copy-done.1
  27.3 0.6 %hand_over.1 = bf16[8,3584]{1,0:T(8,128)(2,1)} custom-call(bf16[8,3584]{1,0:T(8,128)(2,1)S(1)} %attend.1.attn_ref, bf16[8,256,8,256]{3,2,1,0:T(8,128)(2,1)S(1)} %get-tuple-element.26.k_ref, bf16[8,256,8,256]{3,2,1,0:T(8,128)(2,1)S(1)} %get-tuple-element.25.v_ref), custom_call_target="tpu_custom_call" | custom-call | tf_op jit(solution)/shard_map/hand_over/pallas_call | solution.py:383
Async XLA Ops:
  13.3 14.0 %copy-start = (bf16[8,256,8,256]{3,2,1,0:T(8,128)(2,1)}, bf16[8,256,8,256]{3,2,1,0:T(8,128)(2,1)S(1)}, u32[]{:S(2)}) copy-start(bf16[8,256,8,256]{3,2,1,0:T(8,128)(2,1)S(1)} %get-tuple-element.25.v_ref) | copy-start | bytes 25165828
  13.3 14.0 %copy-start.1 = (bf16[8,256,8,256]{3,2,1,0:T(8,128)(2,1)}, bf16[8,256,8,256]{3,2,1,0:T(8,128)(2,1)S(1)}, u32[]{:S(2)}) copy-start(bf16[8,256,8,256]{3,2,1,0:T(8,128)(2,1)S(1)} %get-tuple-element.26.k_ref) | copy-start | bytes 25165828

commit v6 on v5

--- a/solution.py
+++ b/solution.py
@@ -182,8 +182,9 @@
         at_ref[b:b + 1, :] = jnp.full((1, w), wp[b] - me * seq, jnp.int32)
         if b >= EARLY:
             continue
-        s = times(q_ref[b], jnp.concatenate([kn[None]] * TILE, axis=0).reshape(w, dim))
-        f_ref[b] = jnp.where(wp[b] < vl[b], s, -jnp.inf)
+        dots = [jnp.sum(of_row(b, j) * of_row(b, 2), axis=-1, keepdims=True) for j in range(2)]
+        s = jnp.where(wp[b] < vl[b], jnp.concatenate(dots, axis=0) * scale, -jnp.inf)
+        f_ref[b] = jnp.broadcast_to(s, (2 * heads, w))
     for cp in v_copies:
         cp.wait()
 
@@ -217,6 +218,9 @@
     colpos = _positions(heads, w, 2 * seq * n)
     scale = dim ** -0.5
 
+    stats = [jnp.zeros((heads, 128), F32)]
+    own_lane = lax.broadcasted_iota(jnp.int32, (rows, 128), 1) - 4 * lax.broadcasted_iota(jnp.int32, (rows, 128), 0)
+
     def soften(b):
         if b < EARLY:
             at = at_ref[b:b + 1, :]
@@ -233,8 +237,10 @@
         l = jnp.sum(functools.reduce(jnp.add, ps), axis=-1, keepdims=True)
         for t in range(ntile):
             p_ref[b, :, t * w:(t + 1) * w] = ps[t].astype(BF16)
-        st = jnp.where(lane == 0, m[:heads], jnp.where(lane == 1, l[:heads], jnp.where(lane == 2, m[heads:], l[heads:])))
-        xs[pl.ds(blocks * 2 * rows + b, heads, stride=span), :] = st
+        here = (lane // 4) == b
+        part = [m[:heads], l[:heads], m[heads:], l[heads:]]
+        for i, x in enumerate(part):
+            stats[0] = jnp.where(here & (lane % 4 == i), x, stats[0])
 
     def values(b):
         acc = functools.reduce(jnp.add, [
@@ -251,18 +257,22 @@
             soften(i)
         if i >= LAG:
             values(i - LAG)
+    base = blocks * 2 * rows
+    xs[pl.ds(base, heads, stride=span), :] = stats[0]
     pl.semaphore_wait(barrier, n - 1)
-    _exchange(me, n, lambda peer: xs.at[_rows(peer, span)], lambda off: xr.at[off - 1], x2)
+    _exchange(me, n, lambda peer: xs.at[pl.ds(pl.multiple_of(peer * span, span), base + 1)],
+              lambda off: xr.at[off - 1, pl.ds(0, base + 1)], x2)
     xr[n - 1] = xs[_rows(me, span), :]
-    _settle(xr.at[pl.ds(0, n - 1)], x2)
-    base = blocks * 2 * rows
+    _settle(xr.at[pl.ds(0, n - 1), pl.ds(0, base + 1)], x2)
     pieces = []
-    sts = [xr[i, base:base + rows, :] for i in range(n)]
+    def column(i, k):
+        return jnp.sum(jnp.where(own_lane == k, xr[i, base:base + 1, :], 0.0), axis=-1, keepdims=True)
+
     for j in range(2):
-        ms = [st[:, 2 * j:2 * j + 1] for st in sts]
+        ms = [column(i, 2 * j) for i in range(n)]
         top = functools.reduce(jnp.maximum, ms)
         es = [jnp.exp(m - top) for m in ms]
-        total = functools.reduce(jnp.add, [st[:, 2 * j + 1:2 * j + 2] * e for st, e in zip(sts, es)])
+        total = functools.reduce(jnp.add, [column(i, 2 * j + 1) * es[i] for i in range(n)])
         for c in range(blocks):
             at = c * 2 * rows + j * rows
             num = functools.reduce(jnp.add, [xr[i, at:at + rows, :] * es[i] for i in range(n)])

time: 28 us -> 27.8 us (level)
  no operation moved by 1% of the time
where the time goes in v6:
time: 27.8 us; the launch traced here: 27.7 us
  Pallas kernels  25.9 us (93%)
  other arithmetic  1.16 us (4%)
  between operations  0.7 us (3%)
    pallas_call x1, Pallas kernels, local_step(): pl.pallas_call(functools.partial(_attend, n), out_shape=jax.ShapeDtypeStr...  14 us
    pallas_call x1, Pallas kernels, local_step(): pl.pallas_call(functools.partial(_project, n), out_shape=(pltpu.VMEM((EAR...  11.2 us
    min x1, other arithmetic, local_step(): v_next = jnp.minimum(v_here, top)  1.16 us
    pallas_call x1, Pallas kernels, local_step(): pl.pallas_call(_hand_over, out_shape=jax.ShapeDtypeStruct((rows, model),...  0.63 us

profile of v6, /device:TPU:97, one launch (start us, length us, event | category | flops | bytes accessed | tf_op | source)
XLA Modules:
  0.0 27.7 jit_solution(4471528266968696683)
XLA Ops:
  0.6 11.2 %project.1 = (f32[7,16,2048]{2,1,0:T(8,128)S(1)}, f32[7,16,256]{2,1,0:T(8,128)S(1)}, bf16[8,16,256]{2,1,0:T(8,128)(2,1)S(1)}, s32[8,256]{1,0:T(8,128)S(1)}, s32[...) custom-call(bf16[8,3584]{1,0:T(8,128)(2,1)} %hid_ref.1, ...), custom_call_target="tpu_custom_call" | custom-call | flops 10000000000 | bytes 29360128 | tf_op jit(solution)/shard_map/project/pallas_call | solution.py:329
  11.9 0.1 patch.1
  11.9 1.2 %broadcast_minimum_fusion = (bf16[8,256,8,256]{3,2,1,0:T(8,128)(2,1)S(1)}, bf16[8,256,8,256]{3,2,1,0:T(8,128)(2,1)S(1)}) fusion(bf16[8,256,8,256]{3,2,1,0:T(8,128)(2,1)S(1)} %get-tuple-element.24, bf16[]{:T(256)} %constant.0.clone.1, bf16[8,256,8,256]{3,2,1,0:T(8,128)(2,1)S(1)} %get-tuple-element.23), kind=kLoop, calls=%fused_computation | loop fusion | flops 8388608 | bytes 33554432 | tf_op jit(solution)/shard_map/min | solution.py:370
  13.1 0.0 copy-start
  13.1 0.0 copy-start.1
  13.1 14.0 %attend.1.attn_ref = bf16[8,3584]{1,0:T(8,128)(2,1)S(1)} custom-call(f32[7,16,2048]{2,1,0:T(8,128)S(1)} %get-tuple-element.14.s_ref, f32[7,16,256]{2,1,0:T(8,128)S(1)} %get-tuple-element.15.f_ref, bf16[8,16,256]{2,1,0:T(8,128)(2,1)S(1)} %get-tuple-element.16.q_ref, s32[8,256]{1,0:T(8,128)S(1)} %get-tuple-element.17.end_ref, ...), custom_call_target="tpu_custom_call" | custom-call | flops 20000000000 | bytes 4194304 | tf_op jit(solution)/shard_map/attend/pallas_call | solution.py:373
  27.1 0.0 copy-done
  27.1 0.0 copy-done.1
  27.1 0.6 %hand_over.1 = bf16[8,3584]{1,0:T(8,128)(2,1)} custom-call(bf16[8,3584]{1,0:T(8,128)(2,1)S(1)} %attend.1.attn_ref, bf16[8,256,8,256]{3,2,1,0:T(8,128)(2,1)S(1)} %get-tuple-element.26.k_ref, bf16[8,256,8,256]{3,2,1,0:T(8,128)(2,1)S(1)} %get-tuple-element.25.v_ref), custom_call_target="tpu_custom_call" | custom-call | tf_op jit(solution)/shard_map/hand_over/pallas_call | solution.py:393
Async XLA Ops:
  13.1 14.0 %copy-start = (bf16[8,256,8,256]{3,2,1,0:T(8,128)(2,1)}, bf16[8,256,8,256]{3,2,1,0:T(8,128)(2,1)S(1)}, u32[]{:S(2)}) copy-start(bf16[8,256,8,256]{3,2,1,0:T(8,128)(2,1)S(1)} %get-tuple-element.25.v_ref) | copy-start | bytes 25165828
  13.1 14.0 %copy-start.1 = (bf16[8,256,8,256]{3,2,1,0:T(8,128)(2,1)}, bf16[8,256,8,256]{3,2,1,0:T(8,128)(2,1)S(1)}, u32[]{:S(2)}) copy-start(bf16[8,256,8,256]{3,2,1,0:T(8,128)(2,1)S(1)} %get-tuple-element.26.k_ref) | copy-start | bytes 25165828

commit v7 on v6

--- a/solution.py
+++ b/solution.py
@@ -19,7 +19,7 @@
 EARLY = 7
 GROUPS = ((0,), (1, 2), (3, 4), (5, 6))
 TILE = 32
-LAG = 3
+LAG = 2
 MIB = 1 << 20
 
 
@@ -29,7 +29,7 @@
 
 def _greet(me, n):
     barrier = pltpu.get_barrier_semaphore()
-    for off in range(1, n):
+    for off in _far_first(n):
         pl.semaphore_signal(barrier, inc=1, device_id={'sp': _peer(me, off, n)}, device_id_type=MESH)
     return barrier
 
@@ -252,11 +252,12 @@
             xs[pl.ds(c * 2 * rows + b, heads, stride=span), :] = piece[:heads]
             xs[pl.ds(c * 2 * rows + rows + b, heads, stride=span), :] = piece[heads:]
 
+    turn = list(range(EARLY, rows)) + list(range(EARLY))
     for i in range(rows + LAG):
         if i < rows:
-            soften(i)
+            soften(turn[i])
         if i >= LAG:
-            values(i - LAG)
+            values(turn[i - LAG])
     base = blocks * 2 * rows
     xs[pl.ds(base, heads, stride=span), :] = stats[0]
     pl.semaphore_wait(barrier, n - 1)

time: 27.8 us -> 27.8 us (level)
  no operation moved by 1% of the time
where the time goes in v7:
time: 27.8 us; the launch traced here: 27.7 us
  Pallas kernels  25.8 us (93%)
  other arithmetic  1.16 us (4%)
  between operations  0.7 us (3%)
    pallas_call x1, Pallas kernels, local_step(): pl.pallas_call(functools.partial(_attend, n), out_shape=jax.ShapeDtypeStr...  13.9 us
    pallas_call x1, Pallas kernels, local_step(): pl.pallas_call(functools.partial(_project, n), out_shape=(pltpu.VMEM((EAR...  11.2 us
    min x1, other arithmetic, local_step(): v_next = jnp.minimum(v_here, top)  1.16 us
    pallas_call x1, Pallas kernels, local_step(): pl.pallas_call(_hand_over, out_shape=jax.ShapeDtypeStruct((rows, model),...  0.63 us

profile of v7, /device:TPU:97, one launch (start us, length us, event | category | flops | bytes accessed | tf_op | source)
XLA Modules:
  0.0 27.7 jit_solution(12802087490999227931)
XLA Ops:
  0.6 11.2 %project.1 = (f32[7,16,2048]{2,1,0:T(8,128)S(1)}, f32[7,16,256]{2,1,0:T(8,128)S(1)}, bf16[8,16,256]{2,1,0:T(8,128)(2,1)S(1)}, s32[8,256]{1,0:T(8,128)S(1)}, s32[...) custom-call(bf16[8,3584]{1,0:T(8,128)(2,1)} %hid_ref.1, ...), custom_call_target="tpu_custom_call" | custom-call | flops 10000000000 | bytes 29360128 | tf_op jit(solution)/shard_map/project/pallas_call | solution.py:330
  11.9 0.1 patch.1
  11.9 1.2 %broadcast_minimum_fusion = (bf16[8,256,8,256]{3,2,1,0:T(8,128)(2,1)S(1)}, bf16[8,256,8,256]{3,2,1,0:T(8,128)(2,1)S(1)}) fusion(bf16[8,256,8,256]{3,2,1,0:T(8,128)(2,1)S(1)} %get-tuple-element.24, bf16[]{:T(256)} %constant.0.clone.1, bf16[8,256,8,256]{3,2,1,0:T(8,128)(2,1)S(1)} %get-tuple-element.23), kind=kLoop, calls=%fused_computation | loop fusion | flops 8388608 | bytes 33554432 | tf_op jit(solution)/shard_map/min | solution.py:371
  13.1 0.0 copy-start
  13.1 0.0 copy-start.1
  13.1 13.9 %attend.1.attn_ref = bf16[8,3584]{1,0:T(8,128)(2,1)S(1)} custom-call(f32[7,16,2048]{2,1,0:T(8,128)S(1)} %get-tuple-element.14.s_ref, f32[7,16,256]{2,1,0:T(8,128)S(1)} %get-tuple-element.15.f_ref, bf16[8,16,256]{2,1,0:T(8,128)(2,1)S(1)} %get-tuple-element.16.q_ref, s32[8,256]{1,0:T(8,128)S(1)} %get-tuple-element.17.end_ref, ...), custom_call_target="tpu_custom_call" | custom-call | flops 20000000000 | bytes 4194304 | tf_op jit(solution)/shard_map/attend/pallas_call | solution.py:374
  27.0 0.0 copy-done
  27.1 0.0 copy-done.1
  27.1 0.6 %hand_over.1 = bf16[8,3584]{1,0:T(8,128)(2,1)} custom-call(bf16[8,3584]{1,0:T(8,128)(2,1)S(1)} %attend.1.attn_ref, bf16[8,256,8,256]{3,2,1,0:T(8,128)(2,1)S(1)} %get-tuple-element.26.k_ref, bf16[8,256,8,256]{3,2,1,0:T(8,128)(2,1)S(1)} %get-tuple-element.25.v_ref), custom_call_target="tpu_custom_call" | custom-call | tf_op jit(solution)/shard_map/hand_over/pallas_call | solution.py:394
Async XLA Ops:
  13.1 13.9 %copy-start = (bf16[8,256,8,256]{3,2,1,0:T(8,128)(2,1)}, bf16[8,256,8,256]{3,2,1,0:T(8,128)(2,1)S(1)}, u32[]{:S(2)}) copy-start(bf16[8,256,8,256]{3,2,1,0:T(8,128)(2,1)S(1)} %get-tuple-element.25.v_ref) | copy-start | bytes 25165828
  13.1 13.9 %copy-start.1 = (bf16[8,256,8,256]{3,2,1,0:T(8,128)(2,1)}, bf16[8,256,8,256]{3,2,1,0:T(8,128)(2,1)S(1)}, u32[]{:S(2)}) copy-start(bf16[8,256,8,256]{3,2,1,0:T(8,128)(2,1)S(1)} %get-tuple-element.26.k_ref) | copy-start | bytes 25165828

commit v8 on v7

--- a/solution.py
+++ b/solution.py
@@ -210,10 +210,10 @@
     ntile = seq // TILE
     w = TILE * heads
     span = xs.shape[0] // heads
+    barrier = _greet(me, n)
     wcopy = pltpu.make_async_copy(wo_ref, w_ref.at[:, pl.ds(0, model)], wsem)
     wcopy.start()
     w_ref[:, model:] = jnp.zeros((w_ref.shape[0], n * cols - model), BF16)
-    barrier = _greet(me, n)
     lane = lax.broadcasted_iota(jnp.int32, (heads, 128), 1)
     colpos = _positions(heads, w, 2 * seq * n)
     scale = dim ** -0.5

time: 27.8 us -> 27.8 us (level)
  no operation moved by 1% of the time
where the time goes in v8:
time: 27.8 us; the launch traced here: 27.7 us
  Pallas kernels  25.8 us (93%)
  other arithmetic  1.16 us (4%)
  between operations  0.7 us (3%)
    pallas_call x1, Pallas kernels, local_step(): pl.pallas_call(functools.partial(_attend, n), out_shape=jax.ShapeDtypeStr...  13.9 us
    pallas_call x1, Pallas kernels, local_step(): pl.pallas_call(functools.partial(_project, n), out_shape=(pltpu.VMEM((EAR...  11.2 us
    min x1, other arithmetic, local_step(): v_next = jnp.minimum(v_here, top)  1.16 us
    pallas_call x1, Pallas kernels, local_step(): pl.pallas_call(_hand_over, out_shape=jax.ShapeDtypeStruct((rows, model),...  0.63 us

profile of v8, /device:TPU:97, one launch (start us, length us, event | category | flops | bytes accessed | tf_op | source)
XLA Modules:
  0.0 27.7 jit_solution(15569992441534445254)
XLA Ops:
  0.6 11.2 %project.1 = (f32[7,16,2048]{2,1,0:T(8,128)S(1)}, f32[7,16,256]{2,1,0:T(8,128)S(1)}, bf16[8,16,256]{2,1,0:T(8,128)(2,1)S(1)}, s32[8,256]{1,0:T(8,128)S(1)}, s32[...) custom-call(bf16[8,3584]{1,0:T(8,128)(2,1)} %hid_ref.1, ...), custom_call_target="tpu_custom_call" | custom-call | flops 10000000000 | bytes 29360128 | tf_op jit(solution)/shard_map/project/pallas_call | solution.py:330
  11.9 0.1 patch.1
  11.9 1.2 %broadcast_minimum_fusion = (bf16[8,256,8,256]{3,2,1,0:T(8,128)(2,1)S(1)}, bf16[8,256,8,256]{3,2,1,0:T(8,128)(2,1)S(1)}) fusion(bf16[8,256,8,256]{3,2,1,0:T(8,128)(2,1)S(1)} %get-tuple-element.24, bf16[]{:T(256)} %constant.0.clone.1, bf16[8,256,8,256]{3,2,1,0:T(8,128)(2,1)S(1)} %get-tuple-element.23), kind=kLoop, calls=%fused_computation | loop fusion | flops 8388608 | bytes 33554432 | tf_op jit(solution)/shard_map/min | solution.py:371
  13.1 0.0 copy-start
  13.1 0.0 copy-start.1
  13.1 13.9 %attend.1.attn_ref = bf16[8,3584]{1,0:T(8,128)(2,1)S(1)} custom-call(f32[7,16,2048]{2,1,0:T(8,128)S(1)} %get-tuple-element.14.s_ref, f32[7,16,256]{2,1,0:T(8,128)S(1)} %get-tuple-element.15.f_ref, bf16[8,16,256]{2,1,0:T(8,128)(2,1)S(1)} %get-tuple-element.16.q_ref, s32[8,256]{1,0:T(8,128)S(1)} %get-tuple-element.17.end_ref, ...), custom_call_target="tpu_custom_call" | custom-call | flops 20000000000 | bytes 4194304 | tf_op jit(solution)/shard_map/attend/pallas_call | solution.py:374
  27.0 0.0 copy-done
  27.0 0.0 copy-done.1
  27.1 0.6 %hand_over.1 = bf16[8,3584]{1,0:T(8,128)(2,1)} custom-call(bf16[8,3584]{1,0:T(8,128)(2,1)S(1)} %attend.1.attn_ref, bf16[8,256,8,256]{3,2,1,0:T(8,128)(2,1)S(1)} %get-tuple-element.26.k_ref, bf16[8,256,8,256]{3,2,1,0:T(8,128)(2,1)S(1)} %get-tuple-element.25.v_ref), custom_call_target="tpu_custom_call" | custom-call | tf_op jit(solution)/shard_map/hand_over/pallas_call | solution.py:394
Async XLA Ops:
  13.1 13.9 %copy-start = (bf16[8,256,8,256]{3,2,1,0:T(8,128)(2,1)}, bf16[8,256,8,256]{3,2,1,0:T(8,128)(2,1)S(1)}, u32[]{:S(2)}) copy-start(bf16[8,256,8,256]{3,2,1,0:T(8,128)(2,1)S(1)} %get-tuple-element.25.v_ref) | copy-start | bytes 25165828
  13.1 13.9 %copy-start.1 = (bf16[8,256,8,256]{3,2,1,0:T(8,128)(2,1)}, bf16[8,256,8,256]{3,2,1,0:T(8,128)(2,1)S(1)}, u32[]{:S(2)}) copy-start(bf16[8,256,8,256]{3,2,1,0:T(8,128)(2,1)S(1)} %get-tuple-element.26.k_ref) | copy-start | bytes 25165828
